TPU v7x, 32 devices: a whole 2x2x4 slice. The times are simulated.
32 devices in a mesh: space: 8 (over y, x, core), mode: 4 (over z).
Axes of the slice: x: 2, y: 2, z: 4, core: 2. Of those that a mesh axis runs over, the one named last changes fastest.
Arguments:
- occupation_deviation: float32 [2048, 16, 4, 128], P('mode', 'space'), may hold values from -6 to 6
- initial_thermal_offset: float32 [16, 4, 128], P('space'), may hold values from -6 to 6
- branch_specific_warmth: float32 [2048], replicated, may hold values from 0.2 to 2
- courant_numbers: float32 [3, 2048], P(None, 'mode'), may hold values from 0.02 to 0.3
- sign_quadrant: int32 [2048], P('mode'), may hold values from 0 to 7
- scattering_matrix: bfloat16 [2048, 2048], P('mode'), may hold values from -1 to 1
Outputs:
- population_out: float32 [2048, 16, 4, 128], P('mode', 'space')
- thermal_offset: float32 [16, 4, 128], P('space')
All inputs are finite; a program needn't handle non-finite values.
Results may differ from a plain program's by a relative error of at most 0.002.
Values may be sent and summed in bfloat16 or wider, within the bound.
No kernel may reach another device: no remote copies, remote signals or barrier semaphores. Data moves between devices by JAX's collectives and lax.ppermute only.
A program may use at most 64 MiB of HBM per device.

v0:
```python
import jax
import jax.numpy as jnp
from jax import lax
from jax.sharding import PartitionSpec as P

ITERS = 3


def padded_2(cells, sides, width):
    for axis, dim in sides:
        count = lax.axis_size(axis)
        head = lax.slice_in_dim(cells, 0, width, axis=dim)
        tail = lax.slice_in_dim(cells, cells.shape[dim] - width, cells.shape[dim], axis=dim)
        cells = jnp.concatenate(
            [
                lax.ppermute(tail, axis, [(i, (i + 1) % count) for i in range(count)]),
                cells,
                lax.ppermute(head, axis, [((i + 1) % count, i) for i in range(count)]),
            ],
            axis=dim,
        )
    return cells


def advect(lattice_wave_carry, courant_numbers, sign_quadrant):
    padded = padded_2(lattice_wave_carry, (("space", 1),), 1)
    advected = lattice_wave_carry
    for dim_index in range(3):
        if dim_index == 0:
            below_side = padded[:, :-2]
            above_side = padded[:, 2:]
        else:
            below_side = jnp.roll(lattice_wave_carry, 1, dim_index + 1)
            above_side = jnp.roll(lattice_wave_carry, -1, dim_index + 1)
        sign_bit = (sign_quadrant >> dim_index & 1).reshape(-1, 1, 1, 1)
        upwind = jnp.where(sign_bit == 1, above_side, below_side)
        advected = advected - courant_numbers[dim_index].reshape(-1, 1, 1, 1) * (
            lattice_wave_carry - upwind
        )
    return advected


def shards(
    occupation_deviation,
    initial_thermal_offset,
    branch_specific_warmth,
    courant_numbers,
    sign_quadrant,
    scattering_matrix,
):
    local_modes = occupation_deviation.shape[0]
    partition_extents = occupation_deviation.shape
    cell_count = partition_extents[1] * partition_extents[2] * partition_extents[3]
    first_mode = lax.axis_index("mode") * local_modes
    device_specific_warmth = lax.dynamic_slice_in_dim(
        branch_specific_warmth, first_mode, local_modes
    )
    summed_specific_warmth = jnp.sum(branch_specific_warmth)
    lattice_wave_carry = (
        occupation_deviation
        + device_specific_warmth.reshape(-1, 1, 1, 1) * initial_thermal_offset[None]
    )
    scattering_stripes = jnp.dot(
        scattering_matrix.astype(jnp.float32),
        branch_specific_warmth,
        precision=lax.Precision.HIGHEST,
    )
    thermal_offset = jnp.zeros(partition_extents[1:], jnp.float32)
    for iteration in range(ITERS):
        upstream_occupation = advect(lattice_wave_carry, courant_numbers, sign_quadrant)
        moved_bf = upstream_occupation.astype(jnp.bfloat16)
        local_flat_bf = moved_bf.reshape(local_modes, cell_count)
        empty_energy = jnp.zeros((cell_count,), jnp.float32)
        pieces_in = lax.all_gather(moved_bf, "mode", axis=0, tiled=True)
        internal_warmth_field = empty_energy
        piece_rows = pieces_in.shape[0]
        flat_piece = pieces_in.reshape(piece_rows, cell_count)
        scattering_applied = jnp.dot(
            scattering_matrix, flat_piece, preferred_element_type=jnp.float32
        )
        scattering_applied, internal_warmth_field = (scattering_applied, internal_warmth_field)
        local_flat = local_flat_bf.astype(jnp.float32)
        internal_warmth_field = lax.psum(
            jnp.dot(device_specific_warmth, local_flat, precision=lax.Precision.HIGHEST), "mode"
        )
        thermal_offset = (internal_warmth_field / summed_specific_warmth).reshape(
            partition_extents[1:]
        )
        lattice_wave_carry = (
            upstream_occupation
            - scattering_applied.reshape(partition_extents)
            + scattering_stripes.reshape(-1, 1, 1, 1) * thermal_offset[None]
        )
    return (lattice_wave_carry, thermal_offset)


def solution(mesh):
    placed = (
        P("mode", "space", None, None),
        P("space", None, None),
        P(),
        P(None, "mode"),
        P("mode"),
        P("mode", None),
    )
    return jax.shard_map(
        shards,
        mesh=mesh,
        in_specs=placed,
        out_specs=(P("mode", "space", None, None), P("space", None, None)),
        check_vma=False,
    )
```

profile of v0, /device:TPU:0, one launch (start us, length us, event | category | flops | bytes accessed | tf_op | source)
XLA Modules:
  0.0 426.9 jit_solution(6956765198111555662)
XLA Ops:
  8.1 2.7 multiply_add_fusion.3
  11.2 3.4 collective-permute-start
  19.2 18.1 %collective-permute-done = f32[512,1,4,128]{3,2,1,0:T(4,128)S(1)} collective-permute-done((f32[512,1,4,128]{3,2,1,0:T(4,128)S(1)}, f32[512,1,4,128]{3,2,1,0:T(4,128)S(1)}, u32[]{:S(2)}, u32[]{:S(2)}) %collective-permute-start) | collective-permute-done | bytes 1048608 | tf_op jit(solution)/shard_map/ppermute | solution.py:18
  37.3 1.9 collective-permute-done.1
  39.2 9.0 %fusion.34 = (bf16[512,2,4,128]{3,2,1,0:T(4,128)(2,1)}, f32[512,2,4,128]{3,2,1,0:T(4,128)}) fusion(f32[512,2,4,128]{3,2,1,0:T(4,128)S(1)} %multiply_add_fusion.3, f32[512,2,4,127]{3,2,1,0:T(4,128)S(1)} %get-tuple-element.35, f32[512,2,4,1]{3,2,1,0:T(4,128)S(1)} %get-tuple-element.37, f32[512,2,4,1]{3,2,1,0:T(4,128)S(1)} %get-tuple-element.36, ...), kind=kLoop, calls=%fused_computation.54 | loop fusion | flops 9961472 | bytes 15736320 | tf_op jit(solution)/shard_map/convert_element_type | solution.py:71
  52.2 1.7 fusion.54
  53.9 12.5 %psum.21 = f32[1024]{0:T(1024)S(1)} all-reduce(f32[1024]{0:T(1024)S(1)} %bitcast.61), channel_id=1, replica_groups=mesh['space'=8,'mode'=4] {'mode'}, use_global_device_ids=true, to_apply=%region_0.0 | all-reduce | flops 1024 | bytes 8192 | tf_op jit(solution)/shard_map/psum | solution.py:83
  67.1 62.3 %all-gather.4.cloned.1.call-done = bf16[2048,2,4,128]{3,2,1,0:T(4,128)(2,1)} async-done(((bf16[512,2,4,128]{3,2,1,0:T(4,128)(2,1)}), bf16[2048,2,4,128]{3,2,1,0:T(4,128)(2,1)}) %all-gather.4.cloned.1.call-update) | async-done | bytes 4194320 | tf_op jit(solution)/shard_map/all_gather | solution.py:74
  129.4 7.8 %reshape.60 = bf16[2048,1024]{1,0:T(8,128)(2,1)} reshape(bf16[2048,2,4,128]{3,2,1,0:T(4,128)(2,1)} %all-gather.4.cloned.1.call-done) | data formatting | bytes 8388608 | tf_op jit(solution)/shard_map/reshape | solution.py:77
  137.2 5.9 %fusion.52 = f32[1024,512]{1,0:T(8,128)} fusion(bf16[2048,1024]{1,0:T(8,128)(2,1)} %reshape.60, bf16[512,2048]{1,0:T(8,128)(2,1)S(1)} %copy-done), kind=kOutput, calls=%fused_computation.71 | convolution fusion | flops 2147483648 | bytes 8388608 | tf_op jit(solution)/shard_map/dot_general | solution.py:78
  143.1 2.9 copy.11
  146.0 3.1 multiply_add_fusion.2
  155.6 19.7 %collective-permute-done.2 = f32[512,1,4,128]{3,2,1,0:T(4,128)S(1)} collective-permute-done((f32[512,1,4,128]{3,2,1,0:T(4,128)S(1)}, f32[512,1,4,128]{3,2,1,0:T(4,128)S(1)}, u32[]{:S(2)}, u32[]{:S(2)}) %collective-permute-start.2) | collective-permute-done | bytes 1048608 | tf_op jit(solution)/shard_map/ppermute | solution.py:18
  175.4 1.9 collective-permute-done.3
  177.3 8.8 %fusion.32 = (bf16[512,2,4,128]{3,2,1,0:T(4,128)(2,1)}, f32[512,2,4,128]{3,2,1,0:T(4,128)}) fusion(f32[512,2,4,128]{3,2,1,0:T(4,128)S(1)} %multiply_add_fusion.2, f32[512,2,4,127]{3,2,1,0:T(4,128)S(1)} %get-tuple-element.25, f32[512,2,4,1]{3,2,1,0:T(4,128)S(1)} %get-tuple-element.27, f32[512,2,4,1]{3,2,1,0:T(4,128)S(1)} %get-tuple-element.26, ...), kind=kLoop, calls=%fused_computation.53 | loop fusion | flops 9961472 | bytes 15736320 | tf_op jit(solution)/shard_map/convert_element_type | solution.py:71
  186.2 1.8 reshape.65
  188.5 9.5 %psum.22 = f32[1024]{0:T(1024)S(1)} all-reduce(f32[1024]{0:T(1024)S(1)} %bitcast.62), channel_id=1, replica_groups=mesh['space'=8,'mode'=4] {'mode'}, use_global_device_ids=true, to_apply=%region_2.3 | all-reduce | flops 1024 | bytes 8192 | tf_op jit(solution)/shard_map/psum | solution.py:83
  198.6 66.0 %all-gather.6.cloned.1.call-done = bf16[2048,2,4,128]{3,2,1,0:T(4,128)(2,1)} async-done(((bf16[512,2,4,128]{3,2,1,0:T(4,128)(2,1)}), bf16[2048,2,4,128]{3,2,1,0:T(4,128)(2,1)}) %all-gather.6.cloned.1.call-update) | async-done | bytes 4194320 | tf_op jit(solution)/shard_map/all_gather | solution.py:74
  264.6 7.8 %reshape.63 = bf16[2048,1024]{1,0:T(8,128)(2,1)} reshape(bf16[2048,2,4,128]{3,2,1,0:T(4,128)(2,1)} %all-gather.6.cloned.1.call-done) | data formatting | bytes 8388608 | tf_op jit(solution)/shard_map/reshape | solution.py:77
  272.4 5.9 %fusion.55 = f32[1024,512]{1,0:T(8,128)} fusion(bf16[2048,1024]{1,0:T(8,128)(2,1)} %reshape.63, bf16[512,2048]{1,0:T(8,128)(2,1)S(1)} %copy-done), kind=kOutput, calls=%fused_computation.74 | convolution fusion | flops 2147483648 | bytes 8388608 | tf_op jit(solution)/shard_map/dot_general | solution.py:78
  278.3 2.9 copy.12
  281.2 3.1 multiply_add_fusion.1
  290.8 19.7 %collective-permute-done.4 = f32[512,1,4,128]{3,2,1,0:T(4,128)S(1)} collective-permute-done((f32[512,1,4,128]{3,2,1,0:T(4,128)S(1)}, f32[512,1,4,128]{3,2,1,0:T(4,128)S(1)}, u32[]{:S(2)}, u32[]{:S(2)}) %collective-permute-start.4) | collective-permute-done | bytes 1048608 | tf_op jit(solution)/shard_map/ppermute | solution.py:18
  310.6 1.9 collective-permute-done.5
  312.5 8.8 %fusion.30 = (bf16[512,2,4,128]{3,2,1,0:T(4,128)(2,1)}, f32[512,2,4,128]{3,2,1,0:T(4,128)}) fusion(f32[512,2,4,128]{3,2,1,0:T(4,128)S(1)} %multiply_add_fusion.1, f32[512,2,4,127]{3,2,1,0:T(4,128)S(1)} %get-tuple-element.15, f32[512,2,4,1]{3,2,1,0:T(4,128)S(1)} %get-tuple-element.17, f32[512,2,4,1]{3,2,1,0:T(4,128)S(1)} %get-tuple-element.16, ...), kind=kLoop, calls=%fused_computation.52 | loop fusion | flops 9961472 | bytes 15736320 | tf_op jit(solution)/shard_map/convert_element_type | solution.py:71
  321.4 1.8 reshape.68
  323.7 9.4 %psum.23 = f32[1024]{0:T(1024)S(1)} all-reduce(f32[1024]{0:T(1024)S(1)} %bitcast.60), channel_id=1, replica_groups=mesh['space'=8,'mode'=4] {'mode'}, use_global_device_ids=true, to_apply=%region_3.4 | all-reduce | flops 1024 | bytes 8192 | tf_op jit(solution)/shard_map/psum | solution.py:83
  333.8 66.1 %all-gather.8.cloned.1.call-done = bf16[2048,2,4,128]{3,2,1,0:T(4,128)(2,1)} async-done(((bf16[512,2,4,128]{3,2,1,0:T(4,128)(2,1)}), bf16[2048,2,4,128]{3,2,1,0:T(4,128)(2,1)}) %all-gather.8.cloned.1.call-update) | async-done | bytes 4194320 | tf_op jit(solution)/shard_map/all_gather | solution.py:74
  399.8 7.8 %reshape.66 = bf16[2048,1024]{1,0:T(8,128)(2,1)} reshape(bf16[2048,2,4,128]{3,2,1,0:T(4,128)(2,1)} %all-gather.8.cloned.1.call-done) | data formatting | bytes 8388608 | tf_op jit(solution)/shard_map/reshape | solution.py:77
  407.6 5.9 %fusion.57 = f32[1024,512]{1,0:T(8,128)} fusion(bf16[2048,1024]{1,0:T(8,128)(2,1)} %reshape.66, bf16[512,2048]{1,0:T(8,128)(2,1)S(1)} %copy-done), kind=kOutput, calls=%fused_computation.76 | convolution fusion | flops 2147483648 | bytes 8388608 | tf_op jit(solution)/shard_map/dot_general | solution.py:78
  413.5 2.9 copy.13
  416.4 4.0 multiply_add_fusion
  (49 shorter events, 25.9 us)
Async XLA Ops:
  7.2 41.7 %copy-start = (bf16[512,2048]{1,0:T(8,128)(2,1)S(1)}, bf16[512,2048]{1,0:T(8,128)(2,1)}, u32[]{:S(2)}) copy-start(bf16[512,2048]{1,0:T(8,128)(2,1)} %param.11) | copy-start | bytes 6291460
  7.2 122.2 %all-gather.4.cloned.1.call-start = ((), (), s32[]{:S(2)}) async-start(), calls=%async_computation | async-start | bytes 5242880 | tf_op jit(solution)/shard_map/all_gather | solution.py:74
  11.2 26.1 %collective-permute-start = (f32[512,1,4,128]{3,2,1,0:T(4,128)S(1)}, f32[512,1,4,128]{3,2,1,0:T(4,128)S(1)}, u32[]{:S(2)}, u32[]{:S(2)}) collective-permute-start(f32[512,1,4,128]{3,2,1,0:T(4,128)S(1)} %get-tuple-element.28), channel_id=1, source_target_pairs={{4,0},{8,4},{12,8},{16,12},{20,16},{24,20},{28,24},{0,28},{5,1},{9... | collective-permute-start | bytes 3145736 | tf_op jit(solution)/shard_map/ppermute | solution.py:18
  14.7 1.4 copy-start.5
  14.7 1.5 copy-start.4
  14.7 24.6 %collective-permute-start.1 = (f32[512,1,4,128]{3,2,1,0:T(4,128)S(1)}, f32[512,1,4,128]{3,2,1,0:T(4,128)S(1)}, u32[]{:S(2)}, u32[]{:S(2)}) collective-permute-start(f32[512,1,4,128]{3,2,1,0:T(4,128)S(1)} %get-tuple-element.29), channel_id=1, source_target_pairs={{0,4},{4,8},{8,12},{12,16},{16,20},{20,24},{24,28},{28,0},{1,5},{5... | collective-permute-start | bytes 3145736 | tf_op jit(solution)/shard_map/ppermute | solution.py:16
  39.2 9.0 %copy-start.2 = (f32[2048]{0:T(1024)S(1)}, f32[2048]{0:T(1024)}, u32[]{:S(2)}) copy-start(f32[2048]{0:T(1024)} %param.8) | copy-start | bytes 24580
  48.2 2.4 copy-start.1
  48.2 216.4 %all-gather.6.cloned.1.call-start = ((), (), s32[]{:S(2)}) async-start(), calls=%async_computation.1 | async-start | bytes 5242880 | tf_op jit(solution)/shard_map/all_gather | solution.py:74
  150.8 24.5 %collective-permute-start.2 = (f32[512,1,4,128]{3,2,1,0:T(4,128)S(1)}, f32[512,1,4,128]{3,2,1,0:T(4,128)S(1)}, u32[]{:S(2)}, u32[]{:S(2)}) collective-permute-start(f32[512,1,4,128]{3,2,1,0:T(4,128)S(1)} %get-tuple-element.18), channel_id=1, source_target_pairs={{4,0},{8,4},{12,8},{16,12},{20,16},{24,20},{28,24},{0,28},{5,1},{9... | collective-permute-start | bytes 3145736 | tf_op jit(solution)/shard_map/ppermute | solution.py:18
  152.6 24.7 %collective-permute-start.3 = (f32[512,1,4,128]{3,2,1,0:T(4,128)S(1)}, f32[512,1,4,128]{3,2,1,0:T(4,128)S(1)}, u32[]{:S(2)}, u32[]{:S(2)}) collective-permute-start(f32[512,1,4,128]{3,2,1,0:T(4,128)S(1)} %get-tuple-element.19), channel_id=1, source_target_pairs={{0,4},{4,8},{8,12},{12,16},{16,20},{20,24},{24,28},{28,0},{1,5},{5... | collective-permute-start | bytes 3145736 | tf_op jit(solution)/shard_map/ppermute | solution.py:16
  186.2 213.7 %all-gather.8.cloned.1.call-start = ((), (), s32[]{:S(2)}) async-start(), calls=%async_computation.2 | async-start | bytes 5242880 | tf_op jit(solution)/shard_map/all_gather | solution.py:74
  286.0 24.5 %collective-permute-start.4 = (f32[512,1,4,128]{3,2,1,0:T(4,128)S(1)}, f32[512,1,4,128]{3,2,1,0:T(4,128)S(1)}, u32[]{:S(2)}, u32[]{:S(2)}) collective-permute-start(f32[512,1,4,128]{3,2,1,0:T(4,128)S(1)} %get-tuple-element.8), channel_id=1, source_target_pairs={{4,0},{8,4},{12,8},{16,12},{20,16},{24,20},{28,24},{0,28},{5,1},{9... | collective-permute-start | bytes 3145736 | tf_op jit(solution)/shard_map/ppermute | solution.py:18
  287.8 24.7 %collective-permute-start.5 = (f32[512,1,4,128]{3,2,1,0:T(4,128)S(1)}, f32[512,1,4,128]{3,2,1,0:T(4,128)S(1)}, u32[]{:S(2)}, u32[]{:S(2)}) collective-permute-start(f32[512,1,4,128]{3,2,1,0:T(4,128)S(1)} %get-tuple-element.9), channel_id=1, source_target_pairs={{0,4},{4,8},{8,12},{12,16},{16,20},{20,24},{24,28},{28,0},{1,5},{5... | collective-permute-start | bytes 3145736 | tf_op jit(solution)/shard_map/ppermute | solution.py:16
  333.8 82.7 %copy-start.3 = (f32[1024]{0:T(1024)}, f32[1024]{0:T(1024)S(1)}, u32[]{:S(2)}) copy-start(f32[1024]{0:T(1024)S(1)} %broadcast_divide_fusion) | copy-start | bytes 12292
Sparse Core Ops, SparseCore 0:
  48.3 81.0 all-gather.3
  186.3 78.2 all-gather.5
  321.5 78.3 all-gather.7
where the time goes:
time: 428 us; the launch traced here: 427 us
  waiting for transfers between devices  258 us (60%)
  local copies, waits for them, and re-layouts  52.5 us (12%)
  other arithmetic  42.1 us (10%)
  blocking collectives  31.4 us (7%)
  matrix products  22.2 us (5%)
  between operations  14 us (3%)
  starting transfers between devices  7.01 us (2%)
    all_gather x3, waiting for transfers between devices, shards(): pieces_in = lax.all_gather(moved_bf, 'mode', axis=0, tiled=True)  194 us
    ppermute x3, waiting for transfers between devices, padded_2(): lax.ppermute(head, axis, [((i + 1) % count, i) for i in range(count)])  57.6 us
    psum x3, blocking collectives, shards(): lax.psum(jnp.dot(device_specific_warmth, local_flat, precision=lax.Precis...  31.4 us
    convert_element_type x3, other arithmetic, shards(): moved_bf = upstream_occupation.astype(jnp.bfloat16)  26.7 us
    reshape x3, local copies, waits for them, and re-layouts, shards(): flat_piece = pieces_in.reshape(piece_rows, cell_count)  23.3 us
    dot_general x3, matrix products, shards(): jnp.dot(scattering_matrix, flat_piece, preferred_element_type=jnp.float32)  17.7 us
    slice x12, local copies, waits for them, and re-layouts, advect(): above_side = jnp.roll(lattice_wave_carry, -1, dim_index + 1)  13.4 us
    add x3, other arithmetic, shards(): upstream_occupation - scattering_applied.reshape(partition_extents)  10.1 us
  transfers between devices with their start and end apart: 9, of which 9 were waited for; matrix products, arithmetic and copies ran while one was open for 5% of the time, Pallas kernels for 0%

commit v1 on v0

v1 whole, which is shorter than its diff:
```python
import functools
import jax
import jax.numpy as jnp
from jax import lax
from jax.experimental import pallas as pl
from jax.experimental.pallas import tpu as pltpu
from jax.sharding import PartitionSpec as P

ITERS = 3
BOTH = ("space", "mode")
OCTAVES = 31
STEPS = 1024
F32 = jnp.float32
BF16 = jnp.bfloat16


def padded_2(cells, sides, width):
    for axis, dim in sides:
        count = lax.axis_size(axis)
        head = lax.slice_in_dim(cells, 0, width, axis=dim)
        tail = lax.slice_in_dim(cells, cells.shape[dim] - width, cells.shape[dim], axis=dim)
        cells = jnp.concatenate(
            [
                lax.ppermute(tail, axis, [(i, (i + 1) % count) for i in range(count)]),
                cells,
                lax.ppermute(head, axis, [((i + 1) % count, i) for i in range(count)]),
            ],
            axis=dim,
        )
    return cells


def advect(lattice_wave_carry, courant_numbers, sign_quadrant):
    padded = padded_2(lattice_wave_carry, (("space", 1),), 1)
    advected = lattice_wave_carry
    for dim_index in range(3):
        if dim_index == 0:
            below_side = padded[:, :-2]
            above_side = padded[:, 2:]
        else:
            below_side = jnp.roll(lattice_wave_carry, 1, dim_index + 1)
            above_side = jnp.roll(lattice_wave_carry, -1, dim_index + 1)
        sign_bit = (sign_quadrant >> dim_index & 1).reshape(-1, 1, 1, 1)
        upwind = jnp.where(sign_bit == 1, above_side, below_side)
        advected = advected - courant_numbers[dim_index].reshape(-1, 1, 1, 1) * (
            lattice_wave_carry - upwind
        )
    return advected


def plain_shards(occupation, offset, warmth, courant, quadrant, matrix):
    local_modes = occupation.shape[0]
    extents = occupation.shape
    cell_count = extents[1] * extents[2] * extents[3]
    first_mode = lax.axis_index("mode") * local_modes
    own_warmth = lax.dynamic_slice_in_dim(warmth, first_mode, local_modes)
    total_warmth = jnp.sum(warmth)
    state = occupation + own_warmth.reshape(-1, 1, 1, 1) * offset[None]
    relax = jnp.dot(matrix.astype(F32), warmth, precision=lax.Precision.HIGHEST)
    thermal = jnp.zeros(extents[1:], F32)
    for _ in range(ITERS):
        moved = advect(state, courant, quadrant)
        moved_bf = moved.astype(BF16)
        flat = lax.all_gather(moved_bf, "mode", axis=0, tiled=True).reshape(-1, cell_count)
        product = jnp.dot(matrix, flat, preferred_element_type=F32)
        energy = lax.psum(
            jnp.dot(
                own_warmth,
                moved_bf.reshape(local_modes, cell_count).astype(F32),
                precision=lax.Precision.HIGHEST,
            ),
            "mode",
        )
        thermal = (energy / total_warmth).reshape(extents[1:])
        state = moved - product.reshape(extents) + relax.reshape(-1, 1, 1, 1) * thermal[None]
    return state, thermal


def encode(x, inverse):
    y = jnp.maximum(jnp.abs(x) * inverse, 2.0**-OCTAVES)
    e = jnp.clip(jnp.floor(jnp.log2(y)), -float(OCTAVES), -1.0)
    v = (e + (OCTAVES - 1.0)) + y * jnp.exp2(-e)
    code = (v * STEPS + 0.5).astype(jnp.int32)
    return jnp.where(x < 0, -code, code).astype(jnp.int16)


def decode(code, scale):
    c = code.astype(jnp.int32)
    a = jnp.abs(c)
    e = (a >> 10) - OCTAVES
    f = (a & (STEPS - 1)).astype(F32) * (1.0 / STEPS) + 1.0
    v = f * jnp.exp2(e.astype(F32)) * scale
    return jnp.where(a == 0, 0.0, jnp.where(c < 0, -v, v))


def enter_kernel(order, modes, rows, depth, place, occ, offset, warmth, out, work):
    own = warmth[pl.ds(place[0], 1), :]
    for t in range(modes // 128):
        column = jnp.broadcast_to(own[:, t * 128 : t * 128 + 128], (depth, 128)).T
        for q in range(8):
            x = occ[pl.ds(t * 1024 + q, 128, stride=8), :]
            x = x + column * offset[pl.ds(q, 1), :]
            work[t, pl.ds(q, depth, stride=8), :] = x.T
        for k, device in enumerate(order):
            out[device, :, t * 128 : t * 128 + 128] = encode(
                work[t, k * rows : (k + 1) * rows, :], 2.0**-5
            )


def leave_kernel(order, modes, rows, depth, code, aux, out, work):
    cells = aux.shape[2] - 128
    for t in range(modes // 128):
        for k, device in enumerate(order):
            scale = aux[device, :, cells:]
            work[t, k * rows : (k + 1) * rows, :] = decode(
                code[device, :, t * 128 : t * 128 + 128], scale
            )
        for q in range(8):
            x = work[t, pl.ds(q, depth, stride=8), :]
            out[pl.ds(t * 1024 + q, 128, stride=8), :] = x.T


def iterate_kernel(first, last, dims, *refs):
    slices, ring, lane2, modes, blocks = dims
    cells = slices * ring
    width = modes // blocks
    refs = list(refs)
    source, low, high, courant, quadrant, warmth, matrix = refs[:7]
    refs = refs[7:]
    if not first:
        relax_in = refs.pop(0)
    if last:
        code_out, aux_out = refs[:2]
        refs = refs[2:]
    else:
        state_out, low_out, high_out = refs[:3]
        refs = refs[3:]
        if first:
            relax_out = refs.pop(0)
    moved_ref, left, panel, sems = refs[:4]
    state_ref = refs[4] if first else source

    copies = []
    for n in range(blocks):
        copy = pltpu.make_async_copy(
            matrix.at[pl.ds(n * width, width), :], panel.at[n], sems.at[n]
        )
        copy.start()
        copies.append(copy)

    if first:
        spaces = source.shape[0] // blocks
        for s in range(spaces):
            for n in range(blocks):
                x = decode(source[s * blocks + n], 2.0**5)
                for j in range(slices):
                    state_ref[j * ring + s * 8 : j * ring + s * 8 + 8, n * width : (n + 1) * width] = (
                        x[j * 8 : j * 8 + 8]
                    )

    step = 128
    row = lax.broadcasted_iota(jnp.int32, (ring, step), 0) % lane2
    energy = [jnp.zeros((ring, step), F32) for _ in range(slices)]
    largest = jnp.zeros((ring, step), F32)
    capacity = jnp.zeros((1, step), F32)
    for b in range(modes // step):
        at = slice(b * step, (b + 1) * step)
        c = [courant[d : d + 1, at] for d in range(3)]
        sign = quadrant[:, at]
        up = [jnp.broadcast_to((sign >> d & 1) == 1, (ring, step)) for d in range(3)]
        w = warmth[:, at]
        capacity = capacity + w
        x = [state_ref[j * ring : (j + 1) * ring, at] for j in range(slices)]
        if first:
            n, o = divmod(b * step, width)
            lo = jnp.concatenate(
                [low[s * blocks + n, :, o : o + step] for s in range(spaces)], axis=0
            )
            hi = jnp.concatenate(
                [high[s * blocks + n, :, o : o + step] for s in range(spaces)], axis=0
            )
            lo, hi = decode(lo, 2.0**5), decode(hi, 2.0**5)
        else:
            lo, hi = low[:, at].astype(F32), high[:, at].astype(F32)
        around = [lo] + x + [hi]
        for j in range(slices):
            y = x[j]
            below, above = pltpu.roll(y, lane2, 0), pltpu.roll(y, ring - lane2, 0)
            u0 = jnp.where(up[0], above, below)
            below = jnp.where(row == 0, pltpu.roll(y, ring - lane2 + 1, 0), pltpu.roll(y, 1, 0))
            above = jnp.where(
                row == lane2 - 1, pltpu.roll(y, lane2 - 1, 0), pltpu.roll(y, ring - 1, 0)
            )
            u1 = jnp.where(up[1], above, below)
            u2 = jnp.where(up[2], around[j + 2], around[j])
            moved = y - c[0] * (y - u0) - c[1] * (y - u1) - c[2] * (y - u2)
            bf = moved.astype(BF16)
            moved_ref[j * ring : (j + 1) * ring, at] = moved
            left[j * ring : (j + 1) * ring, at] = bf
            energy[j] = energy[j] + w * bf.astype(F32)
            if last:
                largest = jnp.maximum(largest, jnp.abs(moved))
    total = jnp.sum(capacity, axis=1, keepdims=True)
    thermal = jnp.concatenate(
        [jnp.sum(e, axis=1, keepdims=True) for e in energy], axis=0
    ) / total

    if first:
        w = warmth[...]
        w_high = w.astype(BF16)
        w_mid = (w - w_high.astype(F32)).astype(BF16)
        w_low = (w - w_high.astype(F32) - w_mid.astype(F32)).astype(BF16)
        pad = jnp.zeros((13, modes), F32)
        left[cells:, :] = jnp.concatenate(
            [w_high.astype(F32), w_mid.astype(F32), w_low.astype(F32), pad], axis=0
        ).astype(BF16)
    if last:
        peak = jnp.max(jnp.max(largest, axis=1, keepdims=True), axis=0, keepdims=True)
        peak = jnp.maximum(peak, 2.0**-100) * (4.0 * modes)
        flat = jnp.broadcast_to(thermal, (cells, 128)).T
        aux_out[:, :cells] = flat[0:1, :]
        aux_out[:, cells:] = jnp.broadcast_to(peak, (1, 128))
        inverse = 1.0 / peak

    for n in range(blocks):
        at = slice(n * width, (n + 1) * width)
        copies[n].wait()
        product = lax.dot_general(
            left[...], panel[n], (((1,), (1,)), ((), ())), preferred_element_type=F32
        )
        if first:
            relax = product[cells : cells + 1] + product[cells + 1 : cells + 2]
            relax = relax + product[cells + 2 : cells + 3]
            relax_out[:, at] = relax
        else:
            relax = relax_in[:, at]
        state = moved_ref[:, at] - product[:cells] + relax * thermal
        if last:
            for s in range(ring // 8):
                piece = jnp.concatenate(
                    [state[j * ring + s * 8 : j * ring + s * 8 + 8] for j in range(slices)], axis=0
                )
                code_out[s * blocks + n] = encode(piece, inverse)
        else:
            state_out[:, at] = state
            low_out[:, at] = state[:ring].astype(BF16)
            high_out[:, at] = state[cells - ring :].astype(BF16)


def vmem():
    return pl.BlockSpec(memory_space=pltpu.VMEM)


def ring_order(spaces, blocks):
    pairs = max(spaces // 2, 1)
    walk = [q ^ (q >> 1) for q in range(pairs)] if pairs & (pairs - 1) == 0 else list(range(pairs))
    order = []
    for c, q in enumerate(walk):
        for m in range(blocks) if c % 2 == 0 else reversed(range(blocks)):
            for s in range(q * spaces // pairs, (q + 1) * spaces // pairs):
                order.append(s * blocks + m)
    return order


def cell_shards(occupation, offset, warmth, courant, quadrant, matrix):
    spaces, blocks = lax.axis_size("space"), lax.axis_size("mode")
    width, planes, lane2, depth = occupation.shape
    modes = warmth.shape[0]
    slices = depth // (spaces * blocks)
    ring = spaces * planes * lane2
    cells = slices * ring
    rows = slices * 8
    order = ring_order(spaces, blocks)
    count = spaces * blocks
    forward = [(order[k], order[(k + 1) % count]) for k in range(count)]
    backward = [(b, a) for a, b in forward]

    part = width // spaces
    own = lax.dynamic_slice_in_dim(matrix, lax.axis_index("space") * part, part, axis=0)
    full = lax.all_gather(own, ("mode", "space"), axis=0, tiled=True)

    place = lax.axis_index("mode").astype(jnp.int32).reshape(1)
    grid_warmth = warmth.reshape(blocks, width)
    code = pl.pallas_call(
        functools.partial(enter_kernel, order, width, rows, depth),
        out_shape=jax.ShapeDtypeStruct((count, rows, width), jnp.int16),
        in_specs=[pl.BlockSpec(memory_space=pltpu.SMEM), vmem(), vmem(), vmem()],
        out_specs=vmem(),
        scratch_shapes=[pltpu.VMEM((width // 128, depth * 8, 128), F32)],
        name="enter",
    )(place, occupation.reshape(width * 8, depth), offset.reshape(8, depth), grid_warmth)
    source = lax.all_to_all(code, BOTH, 0, 0, tiled=True)
    low_edge, high_edge = source[:, :8], source[:, rows - 8 :]

    row_warmth = warmth.reshape(1, modes)
    all_courant = lax.all_gather(courant, "mode", axis=1, tiled=True)
    all_quadrant = lax.all_gather(quadrant, "mode", axis=0, tiled=True).reshape(1, modes)
    dims = (slices, ring, lane2, modes, blocks)
    edge = jax.ShapeDtypeStruct((ring, modes), BF16)
    relax = None
    for iteration in range(ITERS):
        first, last = iteration == 0, iteration == ITERS - 1
        low = lax.ppermute(high_edge, BOTH, forward)
        high = lax.ppermute(low_edge, BOTH, backward)
        if last:
            outs = (
                jax.ShapeDtypeStruct((count, rows, width), jnp.int16),
                jax.ShapeDtypeStruct((1, cells + 128), F32),
            )
        else:
            outs = (jax.ShapeDtypeStruct((cells, modes), F32), edge, edge)
            if first:
                outs += (jax.ShapeDtypeStruct((1, modes), F32),)
        operands = [source, low, high, all_courant, all_quadrant, row_warmth, full]
        specs = [vmem()] * 6 + [pl.BlockSpec(memory_space=pl.ANY)]
        if not first:
            operands.append(relax)
            specs.append(vmem())
        scratch = [
            pltpu.VMEM((cells, modes), F32),
            pltpu.VMEM((cells + 16 if first else cells, modes), BF16),
            pltpu.VMEM((blocks, width, modes), BF16),
            pltpu.SemaphoreType.DMA((blocks,)),
        ]
        if first:
            scratch.append(pltpu.VMEM((cells, modes), F32))
        results = pl.pallas_call(
            functools.partial(iterate_kernel, first, last, dims),
            out_shape=outs,
            in_specs=specs,
            out_specs=tuple(vmem() for _ in outs),
            scratch_shapes=scratch,
            compiler_params=pltpu.CompilerParams(vmem_limit_bytes=40 * 2**20),
            name=f"iterate{iteration}",
        )(*operands)
        if last:
            code, aux = results
        else:
            source, low_edge, high_edge = results[:3]
            if first:
                relax = results[3]

    aux_all = lax.all_gather(aux, BOTH, axis=0, tiled=False)
    code = lax.all_to_all(code, BOTH, 0, 0, tiled=True)
    population = pl.pallas_call(
        functools.partial(leave_kernel, order, width, rows, depth),
        out_shape=jax.ShapeDtypeStruct((width * 8, depth), F32),
        in_specs=[vmem(), vmem()],
        out_specs=vmem(),
        scratch_shapes=[pltpu.VMEM((width // 128, depth * 8, 128), F32)],
        name="leave",
    )(code, aux_all)
    thermal = aux_all.reshape(count, -1)[jnp.array(order), :cells]
    thermal = thermal.reshape(count, slices, spaces, planes, lane2)
    thermal = lax.dynamic_index_in_dim(thermal, lax.axis_index("space"), 2, keepdims=False)
    thermal = thermal.transpose(2, 3, 0, 1).reshape(planes, lane2, depth)
    return population.reshape(occupation.shape), thermal


def shards(occupation, offset, warmth, courant, quadrant, matrix):
    count = lax.axis_size("space") * lax.axis_size("mode")
    width, planes, lane2, depth = occupation.shape
    fits = (
        depth % count == 0
        and planes * lane2 == 8
        and 8 % lane2 == 0
        and width % 128 == 0
        and width % (16 * lax.axis_size("space")) == 0
        and (depth // count) % 2 == 0
    )
    form = cell_shards if fits else plain_shards
    return form(occupation, offset, warmth, courant, quadrant, matrix)


def solution(mesh):
    placed = (
        P("mode", "space", None, None),
        P("space", None, None),
        P(),
        P(None, "mode"),
        P("mode"),
        P("mode", None),
    )
    return jax.shard_map(
        shards,
        mesh=mesh,
        in_specs=placed,
        out_specs=(P("mode", "space", None, None), P("space", None, None)),
        check_vma=False,
    )
```

time: 428 us -> 301 us (0.70)
  waiting for transfers between devices: 258 us -> 8.13 us
  blocking collectives: 31.4 us -> 149 us
  other arithmetic: 42.1 us -> 0.01 us
  local copies, waits for them, and re-layouts: 52.5 us -> 86.7 us
  Pallas kernels: 0 us -> 32.8 us
  matrix products: 22.2 us -> 0 us
    all_gather x3 -> x1, waiting for transfers between devices: 194 us -> 0.01 us  [cell_shards(): full = lax.all_gather(own, ('mode', 'space'), axis=0, tiled=True)]
    all_gather x0 -> x3, blocking collectives: none -> 101 us  [the longest x1 67.4 us: cell_shards(): aux_all = lax.all_gather(aux, BOTH, axis=0, tiled=False)]
    gather x0 -> x129, local copies, waits for them, and re-layouts: none -> 66.5 us
    ppermute x6, waiting for transfers between devices: 63.3 us -> 8.11 us  [the longest x3 8.1 us: cell_shards(): low = lax.ppermute(high_edge, BOTH, forward)]
    all_to_all x0 -> x1, blocking collectives: none -> 48 us  [cell_shards(): source = lax.all_to_all(code, BOTH, 0, 0, tiled=True)]
    reshape x9 -> x2, local copies, waits for them, and re-layouts: 37.1 us -> 2.02 us  [the longest x1 1.3 us: cell_shards(): grid_warmth = warmth.reshape(blocks, width)]
    pallas_call x0 -> x5, Pallas kernels: none -> 32.8 us  [the longest x3 23.9 us: cell_shards(): pl.pallas_call(functools.partial(iterate_kernel, first, last, dims), out_...]
    psum x3 -> x0, blocking collectives: 31.4 us -> none  [shards(): lax.psum(jnp.dot(device_specific_warmth, local_flat, precision=lax.Precis...]
  transfers between devices with their start and end apart: 9 -> 8, of which waited for: 9 -> 2; matrix products, arithmetic and copies ran while one was open for 5% -> 23% of each run, Pallas kernels for 0% -> 2%
where the time goes in v1:
time: 301 us; the launch traced here: 300 us
  blocking collectives  149 us (50%)
  local copies, waits for them, and re-layouts  86.7 us (29%)
  Pallas kernels  32.8 us (11%)
  between operations  14.2 us (5%)
  starting transfers between devices  8.87 us (3%)
  waiting for transfers between devices  8.13 us (3%)
    all_gather x1, blocking collectives, cell_shards(): aux_all = lax.all_gather(aux, BOTH, axis=0, tiled=False)  67.4 us
    gather x128, local copies, waits for them, and re-layouts  66.4 us
    all_to_all x1, blocking collectives, cell_shards(): source = lax.all_to_all(code, BOTH, 0, 0, tiled=True)  48 us
    pallas_call x3, Pallas kernels, cell_shards(): pl.pallas_call(functools.partial(iterate_kernel, first, last, dims), out_...  23.9 us
    all_gather x1, blocking collectives, cell_shards(): lax.all_gather(quadrant, 'mode', axis=0, tiled=True).reshape(1, modes)  19.7 us
    unnamed x29, local copies, waits for them, and re-layouts  17.3 us
    all_gather x1, blocking collectives, cell_shards(): all_courant = lax.all_gather(courant, 'mode', axis=1, tiled=True)  13.5 us
    ppermute x3, waiting for transfers between devices, cell_shards(): low = lax.ppermute(high_edge, BOTH, forward)  8.1 us
  transfers between devices with their start and end apart: 8, of which 2 were waited for; matrix products, arithmetic and copies ran while one was open for 23% of the time, Pallas kernels for 2%

profile of v1, /device:TPU:0, one launch (start us, length us, event | category | flops | bytes accessed | tf_op | source)
XLA Modules:
  0.0 299.6 jit_solution(16058277970093415617)
XLA Ops:
  7.2 1.5 copy-done
  10.8 4.7 %enter.1 = s16[32,32,512]{2,1,0:T(8,128)(2,1)} custom-call(s32[1]{0:T(128)} %bitcast.place, f32[4096,128]{1,0:T(8,128)} %bitcast.32, f32[8,128]{1,0:T(8,128)} %bitcast.35, f32[4,512]{1,0:T(4,128)} %reshape.37.warmth), custom_call_target="tpu_custom_call" | custom-call | tf_op jit(solution)/shard_map/enter/pallas_call | solution.py:284
  15.5 48.0 %all_to_all.10.refs_0_ = s16[32,32,512]{2,1,0:T(8,128)(2,1)S(1)} all-to-all(s16[32,32,512]{2,1,0:T(8,128)(2,1)} %enter.1), channel_id=1, replica_groups=mesh['space'=8,'mode'=4] {'space','mode'}, dimensions={0} | all-to-all | bytes 2097152 | tf_op jit(solution)/shard_map/all_to_all | solution.py:292
  63.5 1.6 collective-permute-start
  66.2 19.7 %all-gather.1 = s32[4,1,512]{2,1,0:T(1,128)S(1)} all-gather(s32[1,1,512]{2,1,0:T(1,128)S(1)} %bitcast.36), channel_id=1, replica_groups=mesh['space'=8,'mode'=4] {'mode'}, dimensions={0}, use_global_device_ids=true | all-gather | bytes 10240 | tf_op jit(solution)/shard_map/all_gather | solution.py:297
  85.8 13.5 %all_gather.15.refs_3_ = f32[3,2048]{1,0:T(4,128)S(1)} all-gather(f32[3,512]{1,0:T(4,128)S(1)} %copy-done.12), channel_id=1, replica_groups=mesh['space'=8,'mode'=4] {'mode'}, dimensions={1}, use_global_device_ids=true | all-gather | bytes 30720 | tf_op jit(solution)/shard_map/all_gather | solution.py:296
  100.0 3.4 %copy-done.1 = bf16[2048,2048]{1,0:T(8,128)(2,1)S(1)} copy-done((bf16[2048,2048]{1,0:T(8,128)(2,1)S(1)}, bf16[2048,2048]{1,0:T(8,128)(2,1)}, u32[]{:S(2)}) %copy-start.1) | copy-done | bytes 8388632
  104.4 8.8 %iterate0.1 = (f32[256,2048]{1,0:T(8,128)S(1)}, bf16[64,2048]{1,0:T(8,128)(2,1)S(1)}, bf16[64,2048]{1,0:T(8,128)(2,1)S(1)}, f32[1,2048]{1,0:T(1,128)S(1)}) custom-call(s16[32,32,512]{2,1,0:T(8,128)(2,1)S(1)} %all_to_all.10.refs_0_, s16[32,8,512]{2,1,0:T(8,128)(2,1)S(1)} %collective-permute-done.refs_1_, s16[32,8,512]{2,1,0:T(8,128)(2,1)S(1)} %copy-done.7, ...), custom_call_target="tpu_custom_call" | custom-call | tf_op jit(solution)/shard_map/iterate0/pallas_call | solution.py:327
  113.2 1.7 collective-permute-start.3
  114.9 4.0 %collective-permute-done.2.refs_1_ = bf16[64,2048]{1,0:T(8,128)(2,1)S(1)} collective-permute-done((bf16[64,2048]{1,0:T(8,128)(2,1)S(1)}, bf16[64,2048]{1,0:T(8,128)(2,1)S(1)}, u32[]{:S(2)}, u32[]{:S(2)}) %collective-permute-start.2) | collective-permute-done | bytes 262176 | tf_op jit(solution)/shard_map/ppermute | solution.py:303
  119.0 3.4 %copy-done.2 = bf16[2048,2048]{1,0:T(8,128)(2,1)S(1)} copy-done((bf16[2048,2048]{1,0:T(8,128)(2,1)S(1)}, bf16[2048,2048]{1,0:T(8,128)(2,1)}, u32[]{:S(2)}) %copy-start.2) | copy-done | bytes 8388632
  122.4 6.3 %iterate1.1 = (f32[256,2048]{1,0:T(8,128)S(1)}, bf16[64,2048]{1,0:T(8,128)(2,1)S(1)}, bf16[64,2048]{1,0:T(8,128)(2,1)S(1)}) custom-call(f32[256,2048]{1,0:T(8,128)S(1)} %get-tuple-element.11.refs_0_, bf16[64,2048]{1,0:T(8,128)(2,1)S(1)} %collective-permute-done.2.refs_1_, bf16[64,2048]{1,0:T(8,128)(2,1)S(1)} %collective-permute-done.3.refs_2_, ...), custom_call_target="tpu_custom_call" | custom-call | tf_op jit(solution)/shard_map/iterate1/pallas_call | solution.py:327
  131.7 4.0 %collective-permute-done.4.refs_1_ = bf16[64,2048]{1,0:T(8,128)(2,1)S(1)} collective-permute-done((bf16[64,2048]{1,0:T(8,128)(2,1)S(1)}, bf16[64,2048]{1,0:T(8,128)(2,1)S(1)}, u32[]{:S(2)}, u32[]{:S(2)}) %collective-permute-start.4) | collective-permute-done | bytes 262176 | tf_op jit(solution)/shard_map/ppermute | solution.py:303
  135.8 3.4 %copy-done.3 = bf16[2048,2048]{1,0:T(8,128)(2,1)S(1)} copy-done((bf16[2048,2048]{1,0:T(8,128)(2,1)S(1)}, bf16[2048,2048]{1,0:T(8,128)(2,1)}, u32[]{:S(2)}) %copy-start.3) | copy-done | bytes 8388632
  139.2 1.6 copy-done.5
  140.8 8.8 %iterate2.1 = (s16[32,32,512]{2,1,0:T(8,128)(2,1)}, f32[1,384]{1,0:T(1,128)S(1)}) custom-call(f32[256,2048]{1,0:T(8,128)S(1)} %copy-done.5, bf16[64,2048]{1,0:T(8,128)(2,1)S(1)} %collective-permute-done.4.refs_1_, bf16[64,2048]{1,0:T(8,128)(2,1)S(1)} %collective-permute-done.5.refs_2_, f32[3,2048]{1,0:T(4,128)S(1)} %all_gather.15.refs_3_, ...), custom_call_target="tpu_custom_call" | custom-call | tf_op jit(solution)/shard_map/iterate2/pallas_call | solution.py:327
  149.6 67.4 %all-gather.2.aux = f32[32,1,384]{2,1,0:T(1,128)S(1)} all-gather(f32[1,1,384]{2,1,0:T(1,128)S(1)} %bitcast.30), channel_id=2, replica_groups=mesh['space'=8,'mode'=4] {'space','mode'}, dimensions={0}, use_global_device_ids=true | all-gather | bytes 50688 | tf_op jit(solution)/shard_map/all_gather | solution.py:343
  217.0 2.6 all-to-all-start.1
  219.7 66.9 %while.1 = (s32[]{:T(128)}, f32[32,384]{1,0:T(8,128)S(1)}, s32[32,2]{0,1:T(2,128)S(1)}, f32[32,256]{1,0:T(8,128)S(1)}, s32[]{:T(128)}, /*index=5*/s32[]{:T(128)}) while((s32[]{:T(128)}, f32[32,384]{1,0:T(8,128)S(1)}, s32[32,2]{0,1:T(2,128)S(1)}, f32[32,256]{1,0:T(8,128)S(1)}, s32[]{:T(128)}, /*index=5*/s32[]{:T(128)}) %tuple.30), condition=%wide.while_cond, body=%wide.while_body.sunk | while | flops 2 | bytes 4209 | solution.py:353
  220.4 1.4 dynamic-slice.7
  222.5 1.4 dynamic-slice.7
  224.5 1.4 dynamic-slice.7
  226.6 1.4 dynamic-slice.7
  228.7 1.4 dynamic-slice.7
  230.8 1.4 dynamic-slice.7
  232.9 1.4 dynamic-slice.7
  235.0 1.4 dynamic-slice.7
  237.1 1.4 dynamic-slice.7
  241.3 1.4 dynamic-slice.7
  247.5 1.4 dynamic-slice.7
  281.0 1.4 dynamic-slice.7
  288.5 4.2 %leave.1 = f32[4096,128]{1,0:T(8,128)} custom-call(s16[32,32,512]{2,1,0:T(8,128)(2,1)} %copy-done.9, f32[32,1,384]{2,1,0:T(1,128)} %copy-done.10), custom_call_target="tpu_custom_call" | custom-call | tf_op jit(solution)/shard_map/leave/pallas_call | solution.py:345
  (160 shorter events, 59.8 us)
Async XLA Ops:
  7.2 1.6 copy-start
  7.2 92.8 %all-gather.5.cloned.1.call-start = ((), (), s32[]{:S(2)}) async-start(), calls=%async_computation.2 | async-start | bytes 8650752 | tf_op jit(solution)/shard_map/all_gather | solution.py:280
  15.5 50.7 %copy-start.13 = (s32[512]{0:T(512)S(1)}, s32[512]{0:T(512)}, u32[]{:S(2)}) copy-start(s32[512]{0:T(512)} %param.11) | copy-start | bytes 6148
  15.5 70.4 %copy-start.12 = (f32[3,512]{1,0:T(4,128)S(1)}, f32[3,512]{1,0:T(4,128)}, u32[]{:S(2)}) copy-start(f32[3,512]{1,0:T(4,128)} %param.10) | copy-start | bytes 18436
  15.5 84.5 %copy-start.8 = (f32[2048]{0:T(1024)S(1)}, f32[2048]{0:T(1024)}, u32[]{:S(2)}) copy-start(f32[2048]{0:T(1024)} %param.9) | copy-start | bytes 24580
  63.5 35.8 %collective-permute-start = (s16[32,8,512]{2,1,0:T(8,128)(2,1)S(1)}, s16[32,8,512]{2,1,0:T(8,128)(2,1)S(1)}, u32[]{:S(2)}, u32[]{:S(2)}) collective-permute-start(s16[32,8,512]{2,1,0:T(8,128)(2,1)S(1)} %get-tuple-element.39), channel_id=1, source_target_pairs={{0,4},{4,1},{1,5},{5,2},{2,6},{6,3},{3,7},{7,11},{11,15},{15,10},{... | collective-permute-start | bytes 786440 | tf_op jit(solution)/shard_map/ppermute | solution.py:303
  65.1 34.2 %collective-permute-start.1 = (s16[32,8,512]{2,1,0:T(8,128)(2,1)S(1)}, s16[32,8,512]{2,1,0:T(8,128)(2,1)S(1)}, u32[]{:S(2)}, u32[]{:S(2)}) collective-permute-start(s16[32,8,512]{2,1,0:T(8,128)(2,1)S(1)} %get-tuple-element.38), channel_id=1, source_target_pairs={{4,0},{1,4},{5,1},{2,5},{6,2},{3,6},{7,3},{11,7},{15,11},{10,15},{... | collective-permute-start | bytes 786440 | tf_op jit(solution)/shard_map/ppermute | solution.py:304
  99.3 0.7 copy-start.6
  100.0 3.4 %copy-start.1 = (bf16[2048,2048]{1,0:T(8,128)(2,1)S(1)}, bf16[2048,2048]{1,0:T(8,128)(2,1)}, u32[]{:S(2)}) copy-start(bf16[2048,2048]{1,0:T(8,128)(2,1)} %all-gather.5.cloned.1.call-done.refs_6_) | copy-start | bytes 25165828
  103.4 0.9 copy-start.7
  113.1 5.8 %collective-permute-start.2 = (bf16[64,2048]{1,0:T(8,128)(2,1)S(1)}, bf16[64,2048]{1,0:T(8,128)(2,1)S(1)}, u32[]{:S(2)}, u32[]{:S(2)}) collective-permute-start(bf16[64,2048]{1,0:T(8,128)(2,1)S(1)} %get-tuple-element.12), channel_id=1, source_target_pairs={{0,4},{4,1},{1,5},{5,2},{2,6},{6,3},{3,7},{7,11},{11,15},{15,10},{... | collective-permute-start | bytes 786440 | tf_op jit(solution)/shard_map/ppermute | solution.py:303
  113.2 5.8 %collective-permute-start.3 = (bf16[64,2048]{1,0:T(8,128)(2,1)S(1)}, bf16[64,2048]{1,0:T(8,128)(2,1)S(1)}, u32[]{:S(2)}, u32[]{:S(2)}) collective-permute-start(bf16[64,2048]{1,0:T(8,128)(2,1)S(1)} %get-tuple-element.13), channel_id=1, source_target_pairs={{4,0},{1,4},{5,1},{2,5},{6,2},{3,6},{7,3},{11,7},{15,11},{10,15},{... | collective-permute-start | bytes 786440 | tf_op jit(solution)/shard_map/ppermute | solution.py:304
  119.0 3.4 %copy-start.2 = (bf16[2048,2048]{1,0:T(8,128)(2,1)S(1)}, bf16[2048,2048]{1,0:T(8,128)(2,1)}, u32[]{:S(2)}) copy-start(bf16[2048,2048]{1,0:T(8,128)(2,1)} %all-gather.5.cloned.1.call-done.refs_6_) | copy-start | bytes 25165828
  128.7 1.3 copy-start.4
  130.0 5.8 %collective-permute-start.4 = (bf16[64,2048]{1,0:T(8,128)(2,1)S(1)}, bf16[64,2048]{1,0:T(8,128)(2,1)S(1)}, u32[]{:S(2)}, u32[]{:S(2)}) collective-permute-start(bf16[64,2048]{1,0:T(8,128)(2,1)S(1)} %get-tuple-element.16), channel_id=1, source_target_pairs={{0,4},{4,1},{1,5},{5,2},{2,6},{6,3},{3,7},{7,11},{11,15},{15,10},{... | collective-permute-start | bytes 786440 | tf_op jit(solution)/shard_map/ppermute | solution.py:303
  131.3 4.5 %collective-permute-start.5 = (bf16[64,2048]{1,0:T(8,128)(2,1)S(1)}, bf16[64,2048]{1,0:T(8,128)(2,1)S(1)}, u32[]{:S(2)}, u32[]{:S(2)}) collective-permute-start(bf16[64,2048]{1,0:T(8,128)(2,1)S(1)} %get-tuple-element.17), channel_id=1, source_target_pairs={{4,0},{1,4},{5,1},{2,5},{6,2},{3,6},{7,3},{11,7},{15,11},{10,15},{... | collective-permute-start | bytes 786440 | tf_op jit(solution)/shard_map/ppermute | solution.py:304
  135.8 3.4 %copy-start.3 = (bf16[2048,2048]{1,0:T(8,128)(2,1)S(1)}, bf16[2048,2048]{1,0:T(8,128)(2,1)}, u32[]{:S(2)}) copy-start(bf16[2048,2048]{1,0:T(8,128)(2,1)} %all-gather.5.cloned.1.call-done.refs_6_) | copy-start | bytes 25165828
  139.2 1.6 copy-start.5
  149.6 70.1 %copy-start.11 = (s32[32,2]{0,1:T(2,128)S(1)}, s32[32,2]{0,1:T(2,128)}, u32[]{:S(2)}) copy-start(s32[32,2]{0,1:T(2,128)} %constant.49) | copy-start | bytes 772
  217.0 70.6 %copy-start.10 = (f32[32,1,384]{2,1,0:T(1,128)}, f32[32,1,384]{2,1,0:T(1,128)S(1)}, u32[]{:S(2)}) copy-start(f32[32,1,384]{2,1,0:T(1,128)S(1)} %all-gather.2.aux) | copy-start | bytes 147460
  217.0 70.5 %all-to-all-start.1 = ((s16[32,32,512]{2,1,0:T(8,128)(2,1)}), s16[32,32,512]{2,1,0:T(8,128)(2,1)S(1)}, u32[]{:S(2)}, u32[]{:S(2)}) async-start(s16[32,32,512]{2,1,0:T(8,128)(2,1)} %get-tuple-element.18), calls=%async_computation.1 | async-start | bytes 2097152 | tf_op jit(solution)/shard_map/all_to_all | solution.py:344
  287.6 1.0 copy-start.9
Sparse Core Ops, SparseCore 0:
  10.8 88.8 all-gather.4

commit v2 on v1

--- a/solution.py
+++ b/solution.py
@@ -93,70 +93,106 @@
     return jnp.where(a == 0, 0.0, jnp.where(c < 0, -v, v))
 
 
-def enter_kernel(order, modes, rows, depth, place, occ, offset, warmth, out, work):
-    own = warmth[pl.ds(place[0], 1), :]
+def enter_kernel(order, rows, place, occ, offset, warmth, out, work):
+    depth = occ.shape[1]
+    modes = occ.shape[0] // 8
     for t in range(modes // 128):
-        column = jnp.broadcast_to(own[:, t * 128 : t * 128 + 128], (depth, 128)).T
+        at = pl.multiple_of(place[1] * modes + t * 128, 128)
+        column = jnp.broadcast_to(warmth[:, pl.ds(at, 128)], (depth, 128)).T
         for q in range(8):
             x = occ[pl.ds(t * 1024 + q, 128, stride=8), :]
             x = x + column * offset[pl.ds(q, 1), :]
             work[t, pl.ds(q, depth, stride=8), :] = x.T
         for k, device in enumerate(order):
-            out[device, :, t * 128 : t * 128 + 128] = encode(
+            out[device, t * rows : (t + 1) * rows, :] = encode(
                 work[t, k * rows : (k + 1) * rows, :], 2.0**-5
             )
 
 
-def leave_kernel(order, modes, rows, depth, code, aux, out, work):
-    cells = aux.shape[2] - 128
-    for t in range(modes // 128):
+def leave_kernel(order, rows, slices, growth, code, out, thermal_out, work):
+    count = len(order)
+    chunks = work.shape[0]
+    depth = count * slices
+    scales, thermals = [], []
+    for device in order:
+        note = code[device, chunks * rows : chunks * rows + 8, :].astype(jnp.int32)
+        scale = jnp.exp2(note[2:3, :].astype(F32))
+        scales.append(scale * growth)
+        both = decode(note, scale)
+        thermals.append(both[0:1] + both[1:2])
+    flat = jnp.concatenate(thermals, axis=0).T
+    here = lax.broadcasted_iota(jnp.int32, (count, depth), 0) * slices
+    there = lax.broadcasted_iota(jnp.int32, (count, depth), 1)
+    thermal = jnp.zeros((8, depth), F32)
+    for j in range(slices):
+        pick = (here + j == there).astype(F32)
+        thermal = thermal + jnp.dot(
+            flat[j * 8 : j * 8 + 8], pick, precision=lax.Precision.HIGHEST, preferred_element_type=F32
+        )
+    thermal_out[...] = thermal
+    for t in range(chunks):
         for k, device in enumerate(order):
-            scale = aux[device, :, cells:]
             work[t, k * rows : (k + 1) * rows, :] = decode(
-                code[device, :, t * 128 : t * 128 + 128], scale
+                code[device, t * rows : (t + 1) * rows, :], scales[k]
             )
         for q in range(8):
             x = work[t, pl.ds(q, depth, stride=8), :]
             out[pl.ds(t * 1024 + q, 128, stride=8), :] = x.T
 
 
+def collect(place, spaces, blocks, own, parts, full, sems):
+    width = own.shape[0]
+    part = width // spaces
+    s, m = place[0], place[1]
+    pltpu.make_async_copy(own, full.at[pl.ds(m * width, width), :], sems.at[m]).start()
+    for flip, ref in parts:
+        for k in range(1, blocks):
+            n = (m + blocks - k) % blocks
+            to = n * width + (s ^ flip) * part
+            pltpu.make_async_copy(
+                ref.at[pl.ds((k - 1) * part, part), :], full.at[pl.ds(to, part), :], sems.at[n]
+            ).start()
+
+
 def iterate_kernel(first, last, dims, *refs):
-    slices, ring, lane2, modes, blocks = dims
+    slices, ring, lane2, modes, blocks, spaces, flips = dims
     cells = slices * ring
     width = modes // blocks
+    rows = slices * 8
     refs = list(refs)
-    source, low, high, courant, quadrant, warmth, matrix = refs[:7]
-    refs = refs[7:]
-    if not first:
-        relax_in = refs.pop(0)
+    place, source, low, high, warmth = refs[:5]
+    refs = refs[5:]
+    if first:
+        tables, own = refs[:blocks], refs[blocks]
+        parts = list(zip(flips, refs[blocks + 1 : blocks + 1 + len(flips)]))
+        refs = refs[blocks + 1 + len(flips) :]
+    else:
+        table, full, relax_in = refs[:3]
+        refs = refs[3:]
     if last:
-        code_out, aux_out = refs[:2]
-        refs = refs[2:]
+        code_out = refs[0]
+        refs = refs[1:]
     else:
         state_out, low_out, high_out = refs[:3]
         refs = refs[3:]
         if first:
-            relax_out = refs.pop(0)
-    moved_ref, left, panel, sems = refs[:4]
-    state_ref = refs[4] if first else source
-
-    copies = []
-    for n in range(blocks):
-        copy = pltpu.make_async_copy(
-            matrix.at[pl.ds(n * width, width), :], panel.at[n], sems.at[n]
-        )
-        copy.start()
-        copies.append(copy)
-
+            table, full, relax_out = refs[:3]
+            refs = refs[3:]
+    moved_ref, left = refs[:2]
+    state_ref = source
     if first:
-        spaces = source.shape[0] // blocks
+        state_ref, sems = refs[2:]
+        collect(place, spaces, blocks, own, parts, full, sems)
+        for k in range(blocks):
+            n = (place[1] + blocks - k) % blocks
+            table[:, pl.ds(pl.multiple_of(n * width, 128), width)] = tables[k][...]
         for s in range(spaces):
             for n in range(blocks):
-                x = decode(source[s * blocks + n], 2.0**5)
-                for j in range(slices):
-                    state_ref[j * ring + s * 8 : j * ring + s * 8 + 8, n * width : (n + 1) * width] = (
-                        x[j * 8 : j * 8 + 8]
-                    )
+                for t in range(width // 128):
+                    x = decode(source[s * blocks + n, t * rows : (t + 1) * rows, :], 2.0**5)
+                    at = slice(n * width + t * 128, n * width + t * 128 + 128)
+                    for j in range(slices):
+                        state_ref[j * ring + s * 8 : j * ring + s * 8 + 8, at] = x[j * 8 : j * 8 + 8]
 
     step = 128
     row = lax.broadcasted_iota(jnp.int32, (ring, step), 0) % lane2
@@ -165,21 +201,20 @@
     capacity = jnp.zeros((1, step), F32)
     for b in range(modes // step):
         at = slice(b * step, (b + 1) * step)
-        c = [courant[d : d + 1, at] for d in range(3)]
-        sign = quadrant[:, at]
+        c = [table[d : d + 1, at] for d in range(3)]
+        sign = table[3:4, at].astype(jnp.int32)
         up = [jnp.broadcast_to((sign >> d & 1) == 1, (ring, step)) for d in range(3)]
         w = warmth[:, at]
         capacity = capacity + w
         x = [state_ref[j * ring : (j + 1) * ring, at] for j in range(slices)]
         if first:
-            n, o = divmod(b * step, width)
-            lo = jnp.concatenate(
-                [low[s * blocks + n, :, o : o + step] for s in range(spaces)], axis=0
+            n, t = divmod(b, width // step)
+            lo, hi = (
+                decode(
+                    jnp.concatenate([e[s * blocks + n, t] for s in range(spaces)], axis=0), 2.0**5
+                )
+                for e in (low, high)
             )
-            hi = jnp.concatenate(
-                [high[s * blocks + n, :, o : o + step] for s in range(spaces)], axis=0
-            )
-            lo, hi = decode(lo, 2.0**5), decode(hi, 2.0**5)
         else:
             lo, hi = low[:, at].astype(F32), high[:, at].astype(F32)
         around = [lo] + x + [hi]
@@ -216,17 +251,34 @@
         ).astype(BF16)
     if last:
         peak = jnp.max(jnp.max(largest, axis=1, keepdims=True), axis=0, keepdims=True)
-        peak = jnp.maximum(peak, 2.0**-100) * (4.0 * modes)
-        flat = jnp.broadcast_to(thermal, (cells, 128)).T
-        aux_out[:, :cells] = flat[0:1, :]
-        aux_out[:, cells:] = jnp.broadcast_to(peak, (1, 128))
-        inverse = 1.0 / peak
+        power = jnp.ceil(jnp.log2(jnp.maximum(peak, 2.0**-90))) + 1.0
+        inverse = jnp.exp2(-power)
+        turned = jnp.concatenate(
+            [thermal[j * ring + s * 8 : j * ring + s * 8 + 8] for s in range(spaces) for j in range(slices)],
+            axis=0,
+        )
+        flat = jnp.broadcast_to(turned, (cells, 128)).T[0:8, :]
+        coarse = encode(flat, inverse)
+        fine = encode(flat - decode(coarse, jnp.exp2(power)), inverse)
+        coarse, fine = coarse.astype(jnp.int32), fine.astype(jnp.int32)
+        which = lax.broadcasted_iota(jnp.int32, (8, 128), 0)
+        pad = jnp.zeros((8, 128 - rows), jnp.int32)
+        for s in range(spaces):
+            one = jnp.concatenate([coarse[:, s * rows : (s + 1) * rows], pad], axis=1)
+            two = jnp.concatenate([fine[:, s * rows : (s + 1) * rows], pad], axis=1)
+            note = jnp.where(which == 0, one, jnp.where(which == 1, two, power.astype(jnp.int32)))
+            note = note.astype(jnp.int16)
+            for n in range(blocks):
+                code_out[s * blocks + n, width // 128 * rows :, :] = note
+        inverse = inverse * (1.0 / growth_of(modes))
 
     for n in range(blocks):
         at = slice(n * width, (n + 1) * width)
-        copies[n].wait()
+        block = full.at[pl.ds(n * width, width), :]
+        if first:
+            pltpu.make_async_copy(block, block, sems.at[n]).wait()
         product = lax.dot_general(
-            left[...], panel[n], (((1,), (1,)), ((), ())), preferred_element_type=F32
+            left[...], block[...], (((1,), (1,)), ((), ())), preferred_element_type=F32
         )
         if first:
             relax = product[cells : cells + 1] + product[cells + 1 : cells + 2]
@@ -236,15 +288,24 @@
             relax = relax_in[:, at]
         state = moved_ref[:, at] - product[:cells] + relax * thermal
         if last:
-            for s in range(ring // 8):
-                piece = jnp.concatenate(
-                    [state[j * ring + s * 8 : j * ring + s * 8 + 8] for j in range(slices)], axis=0
-                )
-                code_out[s * blocks + n] = encode(piece, inverse)
+            for s in range(spaces):
+                for t in range(width // 128):
+                    piece = jnp.concatenate(
+                        [
+                            state[j * ring + s * 8 : j * ring + s * 8 + 8, t * 128 : t * 128 + 128]
+                            for j in range(slices)
+                        ],
+                        axis=0,
+                    )
+                    code_out[s * blocks + n, t * rows : (t + 1) * rows, :] = encode(piece, inverse)
         else:
             state_out[:, at] = state
             low_out[:, at] = state[:ring].astype(BF16)
             high_out[:, at] = state[cells - ring :].astype(BF16)
+
+
+def growth_of(modes):
+    return 2.0 ** (modes - 1).bit_length() * 4.0
 
 
 def vmem():
@@ -262,6 +323,23 @@
     return order
 
 
+def gather_parts(matrix, spaces, blocks):
+    part = matrix.shape[0] // spaces
+    own = lax.dynamic_slice_in_dim(matrix, lax.axis_index("space") * part, part, axis=0)
+    turns = [[(i, (i + k) % blocks) for i in range(blocks)] for k in range(1, blocks)]
+    arrived = jnp.concatenate([lax.ppermute(own, "mode", turn) for turn in turns], axis=0)
+
+    def flipped(x, flip):
+        return lax.ppermute(x, "space", [(s, s ^ flip) for s in range(spaces)])
+
+    parts = {0: arrived}
+    for flip in range(2, spaces, 2):
+        parts[flip] = flipped(arrived, flip)
+    for flip in range(0, spaces, 2):
+        parts[flip + 1] = flipped(parts[flip], 1)
+    return parts
+
+
 def cell_shards(occupation, offset, warmth, courant, quadrant, matrix):
     spaces, blocks = lax.axis_size("space"), lax.axis_size("mode")
     width, planes, lane2, depth = occupation.shape
@@ -270,98 +348,106 @@
     ring = spaces * planes * lane2
     cells = slices * ring
     rows = slices * 8
+    chunks = width // 128
     order = ring_order(spaces, blocks)
     count = spaces * blocks
     forward = [(order[k], order[(k + 1) % count]) for k in range(count)]
     backward = [(b, a) for a, b in forward]
-
-    part = width // spaces
-    own = lax.dynamic_slice_in_dim(matrix, lax.axis_index("space") * part, part, axis=0)
-    full = lax.all_gather(own, ("mode", "space"), axis=0, tiled=True)
-
-    place = lax.axis_index("mode").astype(jnp.int32).reshape(1)
-    grid_warmth = warmth.reshape(blocks, width)
+    place = jnp.stack([lax.axis_index("space"), lax.axis_index("mode")]).astype(jnp.int32)
+    row_warmth = warmth.reshape(1, modes)
+
+    parts = gather_parts(matrix, spaces, blocks)
+    table = jnp.concatenate([courant, quadrant.astype(F32).reshape(1, width)], axis=0)
+    tables = [table] + [
+        lax.ppermute(table, "mode", [(i, (i + k) % blocks) for i in range(blocks)])
+        for k in range(1, blocks)
+    ]
+
+    smem = pl.BlockSpec(memory_space=pltpu.SMEM)
+    anywhere = pl.BlockSpec(memory_space=pl.ANY)
     code = pl.pallas_call(
-        functools.partial(enter_kernel, order, width, rows, depth),
-        out_shape=jax.ShapeDtypeStruct((count, rows, width), jnp.int16),
-        in_specs=[pl.BlockSpec(memory_space=pltpu.SMEM), vmem(), vmem(), vmem()],
+        functools.partial(enter_kernel, order, rows),
+        out_shape=jax.ShapeDtypeStruct((count, chunks * rows, 128), jnp.int16),
+        in_specs=[smem, vmem(), vmem(), vmem()],
         out_specs=vmem(),
-        scratch_shapes=[pltpu.VMEM((width // 128, depth * 8, 128), F32)],
+        scratch_shapes=[pltpu.VMEM((chunks, depth * 8, 128), F32)],
         name="enter",
-    )(place, occupation.reshape(width * 8, depth), offset.reshape(8, depth), grid_warmth)
+    )(place, occupation.reshape(width * 8, depth), offset.reshape(8, depth), row_warmth)
+    code, parts[0] = lax.optimization_barrier((code, parts[0]))
     source = lax.all_to_all(code, BOTH, 0, 0, tiled=True)
-    low_edge, high_edge = source[:, :8], source[:, rows - 8 :]
-
-    row_warmth = warmth.reshape(1, modes)
-    all_courant = lax.all_gather(courant, "mode", axis=1, tiled=True)
-    all_quadrant = lax.all_gather(quadrant, "mode", axis=0, tiled=True).reshape(1, modes)
-    dims = (slices, ring, lane2, modes, blocks)
+    split = source.reshape(count, chunks, rows, 128)
+    low_edge, high_edge = split[:, :, :8], split[:, :, rows - 8 :]
+
+    flips = tuple(sorted(parts))
+    dims = (slices, ring, lane2, modes, blocks, spaces, flips)
     edge = jax.ShapeDtypeStruct((ring, modes), BF16)
-    relax = None
+    whole = (
+        jax.ShapeDtypeStruct((4, modes), F32),
+        jax.ShapeDtypeStruct((modes, modes), BF16),
+        jax.ShapeDtypeStruct((1, modes), F32),
+    )
+    kept = ()
     for iteration in range(ITERS):
         first, last = iteration == 0, iteration == ITERS - 1
         low = lax.ppermute(high_edge, BOTH, forward)
         high = lax.ppermute(low_edge, BOTH, backward)
         if last:
-            outs = (
-                jax.ShapeDtypeStruct((count, rows, width), jnp.int16),
-                jax.ShapeDtypeStruct((1, cells + 128), F32),
-            )
+            outs = (jax.ShapeDtypeStruct((count, chunks * rows + 8, 128), jnp.int16),)
         else:
             outs = (jax.ShapeDtypeStruct((cells, modes), F32), edge, edge)
             if first:
-                outs += (jax.ShapeDtypeStruct((1, modes), F32),)
-        operands = [source, low, high, all_courant, all_quadrant, row_warmth, full]
-        specs = [vmem()] * 6 + [pl.BlockSpec(memory_space=pl.ANY)]
-        if not first:
-            operands.append(relax)
-            specs.append(vmem())
+                outs += whole
+        operands = [place, source, low, high, row_warmth]
+        specs = [smem] + [vmem()] * 4
         scratch = [
             pltpu.VMEM((cells, modes), F32),
             pltpu.VMEM((cells + 16 if first else cells, modes), BF16),
-            pltpu.VMEM((blocks, width, modes), BF16),
-            pltpu.SemaphoreType.DMA((blocks,)),
         ]
         if first:
-            scratch.append(pltpu.VMEM((cells, modes), F32))
+            operands += tables + [matrix] + [parts[f] for f in flips]
+            specs += [vmem()] * blocks + [anywhere] * (1 + len(flips))
+            scratch += [pltpu.VMEM((cells, modes), F32), pltpu.SemaphoreType.DMA((blocks,))]
+        else:
+            operands += kept
+            specs += [vmem()] * 3
         results = pl.pallas_call(
             functools.partial(iterate_kernel, first, last, dims),
             out_shape=outs,
             in_specs=specs,
             out_specs=tuple(vmem() for _ in outs),
             scratch_shapes=scratch,
-            compiler_params=pltpu.CompilerParams(vmem_limit_bytes=40 * 2**20),
+            compiler_params=pltpu.CompilerParams(vmem_limit_bytes=30 * 2**20),
             name=f"iterate{iteration}",
         )(*operands)
         if last:
-            code, aux = results
+            code = results[0]
         else:
             source, low_edge, high_edge = results[:3]
-            if first:
-                relax = results[3]
-
-    aux_all = lax.all_gather(aux, BOTH, axis=0, tiled=False)
+            kept = kept or results[3:]
+
     code = lax.all_to_all(code, BOTH, 0, 0, tiled=True)
-    population = pl.pallas_call(
-        functools.partial(leave_kernel, order, width, rows, depth),
-        out_shape=jax.ShapeDtypeStruct((width * 8, depth), F32),
-        in_specs=[vmem(), vmem()],
-        out_specs=vmem(),
-        scratch_shapes=[pltpu.VMEM((width // 128, depth * 8, 128), F32)],
+    population, thermal = pl.pallas_call(
+        functools.partial(leave_kernel, order, rows, slices, growth_of(modes)),
+        out_shape=(
+            jax.ShapeDtypeStruct((width * 8, depth), F32),
+            jax.ShapeDtypeStruct((8, depth), F32),
+        ),
+        in_specs=[vmem()],
+        out_specs=(vmem(), vmem()),
+        scratch_shapes=[pltpu.VMEM((chunks, depth * 8, 128), F32)],
         name="leave",
-    )(code, aux_all)
-    thermal = aux_all.reshape(count, -1)[jnp.array(order), :cells]
-    thermal = thermal.reshape(count, slices, spaces, planes, lane2)
-    thermal = lax.dynamic_index_in_dim(thermal, lax.axis_index("space"), 2, keepdims=False)
-    thermal = thermal.transpose(2, 3, 0, 1).reshape(planes, lane2, depth)
-    return population.reshape(occupation.shape), thermal
+    )(code)
+    return population.reshape(occupation.shape), thermal.reshape(offset.shape)
 
 
 def shards(occupation, offset, warmth, courant, quadrant, matrix):
     count = lax.axis_size("space") * lax.axis_size("mode")
     width, planes, lane2, depth = occupation.shape
     fits = (
-        depth % count == 0
+        depth == 128
+        and depth % count == 0
+        and lax.axis_size("space") & (lax.axis_size("space") - 1) == 0
+        and lax.axis_size("space") > 1
         and planes * lane2 == 8
         and 8 % lane2 == 0
         and width % 128 == 0

time: 301 us -> 177 us (0.59)
  blocking collectives: 149 us -> 34.5 us
  local copies, waits for them, and re-layouts: 86.7 us -> 3.25 us
  waiting for transfers between devices: 8.13 us -> 82.7 us
  starting transfers between devices: 8.87 us -> 24.4 us
  between operations: 14.2 us -> 0.72 us
    all_gather x3 -> x0, blocking collectives: 101 us -> none  [the longest x1 67.4 us: cell_shards(): aux_all = lax.all_gather(aux, BOTH, axis=0, tiled=False)]
    ppermute x0 -> x13, waiting for transfers between devices: none -> 69.3 us  [the longest x7 45.1 us: flipped(): return lax.ppermute(x, 'space', [(s, s ^ flip) for s in range(spaces)])]
    gather x129 -> x0, local copies, waits for them, and re-layouts: 66.5 us -> none
    ppermute x0 -> x13, starting transfers between devices: none -> 16.4 us  [the longest x3 6.63 us: cell_shards(): lax.ppermute(table, 'mode', [(i, (i + k) % blocks) for i in range(blocks)])]
    unnamed x29 -> x12, local copies, waits for them, and re-layouts: 17.3 us -> 1.47 us
    all_to_all x1, blocking collectives: 48 us -> 34.5 us  [cell_shards(): code = lax.all_to_all(code, BOTH, 0, 0, tiled=True)]
    ppermute x3, waiting for transfers between devices: 0.01 us -> 3.37 us  [cell_shards(): high = lax.ppermute(low_edge, BOTH, backward)]
  transfers between devices with their start and end apart: 8 -> 20, of which waited for: 2 -> 12; matrix products, arithmetic and copies ran while one was open for 23% -> 1% of each run, Pallas kernels for 2% -> 3%
where the time goes in v2:
time: 177 us
  waiting for transfers between devices  82.7 us (47%)
  blocking collectives  34.5 us (19%)
  Pallas kernels  30.7 us (17%)
  starting transfers between devices  24.4 us (14%)
  local copies, waits for them, and re-layouts  3.25 us (2%)
    ppermute x7, waiting for transfers between devices, flipped(): return lax.ppermute(x, 'space', [(s, s ^ flip) for s in range(spaces)])  45.1 us
    all_to_all x1, blocking collectives, cell_shards(): code = lax.all_to_all(code, BOTH, 0, 0, tiled=True)  34.5 us
    pallas_call x3, Pallas kernels, cell_shards(): pl.pallas_call(functools.partial(iterate_kernel, first, last, dims), out_...  21.6 us
    ppermute x3, waiting for transfers between devices, gather_parts(): lax.ppermute(own, 'mode', turn)  16.1 us
    ppermute x3, waiting for transfers between devices, cell_shards(): low = lax.ppermute(high_edge, BOTH, forward)  9.95 us
    ppermute x3, waiting for transfers between devices, cell_shards(): lax.ppermute(table, 'mode', [(i, (i + k) % blocks) for i in range(blocks)])  8.11 us
    ppermute x3, starting transfers between devices, cell_shards(): lax.ppermute(table, 'mode', [(i, (i + k) % blocks) for i in range(blocks)])  6.63 us
    ppermute x3, starting transfers between devices, gather_parts(): lax.ppermute(own, 'mode', turn)  6.14 us
  transfers between devices with their start and end apart: 20, of which 12 were waited for; matrix products, arithmetic and copies ran while one was open for 1% of the time, Pallas kernels for 3%

profile of v2, /device:TPU:0, one launch (start us, length us, event | category | flops | bytes accessed | tf_op | source)
XLA Modules:
  0.0 176.8 jit_solution(7349093286005778561)
XLA Ops:
  0.6 1.0 constant_dynamic-slice_fusion
  1.6 3.1 %collective-permute-start = (bf16[64,2048]{1,0:T(8,128)(2,1)S(1)}, bf16[64,2048]{1,0:T(8,128)(2,1)S(1)}, u32[]{:S(2)}, u32[]{:S(2)}) collective-permute-start(bf16[64,2048]{1,0:T(8,128)(2,1)S(1)} %constant_dynamic-slice_fusion), channel_id=1, source_target_pairs={{0,1},{1,2},{2,3},{3,0},{4,5},{5,6},{6,7},{7,4},{8,9},{9,10},{10,1... | collective-permute-start | bytes 786440 | tf_op jit(solution)/shard_map/ppermute | solution.py:330
  4.7 2.1 %collective-permute-start.2 = (bf16[64,2048]{1,0:T(8,128)(2,1)S(1)}, bf16[64,2048]{1,0:T(8,128)(2,1)S(1)}, u32[]{:S(2)}, u32[]{:S(2)}) collective-permute-start(bf16[64,2048]{1,0:T(8,128)(2,1)S(1)} %constant_dynamic-slice_fusion), channel_id=1, source_target_pairs={{0,3},{1,0},{2,1},{3,2},{4,7},{5,4},{6,5},{7,6},{8,11},{9,8},{10,9... | collective-permute-start | bytes 786440 | tf_op jit(solution)/shard_map/ppermute | solution.py:330
  6.8 0.9 collective-permute-start.1
  7.8 0.6 pad_add_fusion.place.refs_0_
  8.4 4.7 %enter.1 = s16[32,128,128]{2,1,0:T(8,128)(2,1)} custom-call(s32[2]{0:T(128)} %pad_add_fusion.place.refs_0_, f32[4096,128]{1,0:T(8,128)} %bitcast.14, f32[8,128]{1,0:T(8,128)} %bitcast.16, f32[1,2048]{1,0:T(1,128)} %bitcast.10), custom_call_target="tpu_custom_call" | custom-call | tf_op jit(solution)/shard_map/enter/pallas_call | solution.py:368
  13.0 0.9 collective-permute-done
  13.9 0.7 constant_dynamic-update-slice_fusion.2
  14.7 15.2 %collective-permute-done.1 = bf16[64,2048]{1,0:T(8,128)(2,1)S(1)} collective-permute-done((bf16[64,2048]{1,0:T(8,128)(2,1)S(1)}, bf16[64,2048]{1,0:T(8,128)(2,1)S(1)}, u32[]{:S(2)}, u32[]{:S(2)}) %collective-permute-start.1) | collective-permute-done | bytes 262176 | tf_op jit(solution)/shard_map/ppermute | solution.py:330
  29.9 0.7 constant_dynamic-update-slice_fusion.1
  30.6 0.7 constant_dynamic-update-slice_fusion.refs_10_
  31.3 3.9 %all-to-all-start = ((s16[32,128,128]{2,1,0:T(8,128)(2,1)}), s16[32,128,128]{2,1,0:T(8,128)(2,1)S(1)}, u32[]{:S(2)}, u32[]{:S(2)}) async-start(s16[32,128,128]{2,1,0:T(8,128)(2,1)} %enter.1), calls=%async_computation | async-start | bytes 2097152 | tf_op jit(solution)/shard_map/all_to_all | solution.py:377
  35.2 2.7 %collective-permute-start.13 = (bf16[192,2048]{1,0:T(8,128)(2,1)}, bf16[192,2048]{1,0:T(8,128)(2,1)}, u32[]{:S(2)}, u32[]{:S(2)}) collective-permute-start(bf16[192,2048]{1,0:T(8,128)(2,1)} %constant_dynamic-update-slice_fusion.refs_10_), channel_id=1, source_target_pairs={{0,24},{4,28},{8,16},{12,20},{16,8},{20,12},{24,0},{28,4},{1,25},{... | collective-permute-start | bytes 2359304 | tf_op jit(solution)/shard_map/ppermute | solution.py:333
  38.8 29.7 %collective-permute-done.13.refs_16_ = bf16[192,2048]{1,0:T(8,128)(2,1)} collective-permute-done((bf16[192,2048]{1,0:T(8,128)(2,1)}, bf16[192,2048]{1,0:T(8,128)(2,1)}, u32[]{:S(2)}, u32[]{:S(2)}) %collective-permute-start.13) | collective-permute-done | bytes 786464 | tf_op jit(solution)/shard_map/ppermute | solution.py:333
  68.5 14.9 %collective-permute-done.11.refs_14_ = bf16[192,2048]{1,0:T(8,128)(2,1)} collective-permute-done((bf16[192,2048]{1,0:T(8,128)(2,1)}, bf16[192,2048]{1,0:T(8,128)(2,1)}, u32[]{:S(2)}, u32[]{:S(2)}) %collective-permute-start.11) | collective-permute-done | bytes 786464 | tf_op jit(solution)/shard_map/ppermute | solution.py:333
  83.9 3.2 %collective-permute-start.7 = (f32[4,512]{1,0:T(4,128)S(1)}, f32[4,512]{1,0:T(4,128)S(1)}, u32[]{:S(2)}, u32[]{:S(2)}) collective-permute-start(f32[4,512]{1,0:T(4,128)S(1)} %pad_maximum_fusion.refs_5_), channel_id=1, source_target_pairs={{0,3},{1,0},{2,1},{3,2},{4,7},{5,4},{6,5},{7,6},{8,11},{9,8},{10,9... | collective-permute-start | bytes 24584 | tf_op jit(solution)/shard_map/ppermute | solution.py:362
  87.2 1.4 collective-permute-done.7.refs_8_
  88.5 1.7 collective-permute-start.6
  90.2 2.9 %collective-permute-done.6.refs_7_ = f32[4,512]{1,0:T(4,128)S(1)} collective-permute-done((f32[4,512]{1,0:T(4,128)S(1)}, f32[4,512]{1,0:T(4,128)S(1)}, u32[]{:S(2)}, u32[]{:S(2)}) %collective-permute-start.6) | collective-permute-done | bytes 8224 | tf_op jit(solution)/shard_map/ppermute | solution.py:362
  93.1 1.7 collective-permute-start.5
  94.9 3.9 %collective-permute-done.5.refs_6_ = f32[4,512]{1,0:T(4,128)S(1)} collective-permute-done((f32[4,512]{1,0:T(4,128)S(1)}, f32[4,512]{1,0:T(4,128)S(1)}, u32[]{:S(2)}, u32[]{:S(2)}) %collective-permute-start.5) | collective-permute-done | bytes 8224 | tf_op jit(solution)/shard_map/ppermute | solution.py:362
  99.3 3.4 %collective-permute-done.4.refs_3_ = s16[32,4,8,128]{3,2,1,0:T(8,128)(2,1)S(1)} collective-permute-done((s16[32,4,8,128]{3,2,1,0:T(8,128)(2,1)S(1)}, s16[32,4,8,128]{3,2,1,0:T(8,128)(2,1)S(1)}, u32[]{:S(2)}, u32[]{:S(2)}) %collective-permute-start.4) | collective-permute-done | bytes 262176 | tf_op jit(solution)/shard_map/ppermute | solution.py:393
  102.7 1.9 %collective-permute-done.3.refs_2_ = s16[32,4,8,128]{3,2,1,0:T(8,128)(2,1)S(1)} collective-permute-done((s16[32,4,8,128]{3,2,1,0:T(8,128)(2,1)S(1)}, s16[32,4,8,128]{3,2,1,0:T(8,128)(2,1)S(1)}, u32[]{:S(2)}, u32[]{:S(2)}) %collective-permute-start.3) | collective-permute-done | bytes 262176 | tf_op jit(solution)/shard_map/ppermute | solution.py:392
  104.6 9.7 %iterate0.1 = (f32[256,2048]{1,0:T(8,128)S(1)}, bf16[64,2048]{1,0:T(8,128)(2,1)S(1)}, bf16[64,2048]{1,0:T(8,128)(2,1)S(1)}, f32[4,2048]{1,0:T(4,128)S(1)}, bf16[...) custom-call(s32[2]{0:T(128)S(1)} %copy-done.2, s16[32,128,128]{2,1,0:T(8,128)(2,1)S(1)} %all-to-all-done.refs_1_, ...), custom_call_target="tpu_custom_call" | custom-call | tf_op jit(solution)/shard_map/iterate0/pallas_call | solution.py:413
  114.4 1.7 collective-permute-start.16
  116.1 4.0 %collective-permute-done.15.refs_2_ = bf16[64,2048]{1,0:T(8,128)(2,1)S(1)} collective-permute-done((bf16[64,2048]{1,0:T(8,128)(2,1)S(1)}, bf16[64,2048]{1,0:T(8,128)(2,1)S(1)}, u32[]{:S(2)}, u32[]{:S(2)}) %collective-permute-start.15) | collective-permute-done | bytes 262176 | tf_op jit(solution)/shard_map/ppermute | solution.py:392
  120.2 5.2 %iterate1.1 = (f32[256,2048]{1,0:T(8,128)S(1)}, bf16[64,2048]{1,0:T(8,128)(2,1)S(1)}, bf16[64,2048]{1,0:T(8,128)(2,1)S(1)}) custom-call(s32[2]{0:T(128)S(1)} %copy-done.2, f32[256,2048]{1,0:T(8,128)S(1)} %get-tuple-element.17.refs_1_, bf16[64,2048]{1,0:T(8,128)(2,1)S(1)} %collective-permute-done.15.refs_2_, ...), custom_call_target="tpu_custom_call" | custom-call | tf_op jit(solution)/shard_map/iterate1/pallas_call | solution.py:413
  125.4 1.3 collective-permute-start.17
  127.3 4.0 %collective-permute-done.17.refs_2_ = bf16[64,2048]{1,0:T(8,128)(2,1)S(1)} collective-permute-done((bf16[64,2048]{1,0:T(8,128)(2,1)S(1)}, bf16[64,2048]{1,0:T(8,128)(2,1)S(1)}, u32[]{:S(2)}, u32[]{:S(2)}) %collective-permute-start.17) | collective-permute-done | bytes 262176 | tf_op jit(solution)/shard_map/ppermute | solution.py:392
  131.3 6.7 %iterate2.1 = s16[32,136,128]{2,1,0:T(8,128)(2,1)S(1)} custom-call(s32[2]{0:T(128)S(1)} %copy-done.2, f32[256,2048]{1,0:T(8,128)S(1)} %get-tuple-element.23.refs_1_, bf16[64,2048]{1,0:T(8,128)(2,1)S(1)} %collective-permute-done.17.refs_2_, bf16[64,2048]{1,0:T(8,128)(2,1)S(1)} %collective-permute-done.18.refs_3_, f32[1,2048]{1,0:T(1,128)S(1)} %bitcast.13, ...), custom_call_target="tpu_custom_call" | custom-call | tf_op jit(solution)/shard_map/iterate2/pallas_call | solution.py:413
  138.0 34.5 %all_to_all.10.code = s16[32,136,128]{2,1,0:T(8,128)(2,1)} all-to-all(s16[32,136,128]{2,1,0:T(8,128)(2,1)S(1)} %iterate2.1), channel_id=1, replica_groups=mesh['space'=8,'mode'=4] {'space','mode'}, dimensions={0} | all-to-all | bytes 2228224 | tf_op jit(solution)/shard_map/all_to_all | solution.py:428
  172.5 4.4 %leave.1 = (f32[4096,128]{1,0:T(8,128)}, f32[8,128]{1,0:T(8,128)}) custom-call(s16[32,136,128]{2,1,0:T(8,128)(2,1)} %all_to_all.10.code), custom_call_target="tpu_custom_call" | custom-call | tf_op jit(solution)/shard_map/leave/pallas_call | solution.py:429
  (32 shorter events, 2.6 us)
Async XLA Ops:
  1.6 12.3 %collective-permute-start = (bf16[64,2048]{1,0:T(8,128)(2,1)S(1)}, bf16[64,2048]{1,0:T(8,128)(2,1)S(1)}, u32[]{:S(2)}, u32[]{:S(2)}) collective-permute-start(bf16[64,2048]{1,0:T(8,128)(2,1)S(1)} %constant_dynamic-slice_fusion), channel_id=1, source_target_pairs={{0,1},{1,2},{2,3},{3,0},{4,5},{5,6},{6,7},{7,4},{8,9},{9,10},{10,1... | collective-permute-start | bytes 786440 | tf_op jit(solution)/shard_map/ppermute | solution.py:330
  4.7 25.9 %collective-permute-start.2 = (bf16[64,2048]{1,0:T(8,128)(2,1)S(1)}, bf16[64,2048]{1,0:T(8,128)(2,1)S(1)}, u32[]{:S(2)}, u32[]{:S(2)}) collective-permute-start(bf16[64,2048]{1,0:T(8,128)(2,1)S(1)} %constant_dynamic-slice_fusion), channel_id=1, source_target_pairs={{0,3},{1,0},{2,1},{3,2},{4,7},{5,4},{6,5},{7,6},{8,11},{9,8},{10,9... | collective-permute-start | bytes 786440 | tf_op jit(solution)/shard_map/ppermute | solution.py:330
  6.8 23.1 %collective-permute-start.1 = (bf16[64,2048]{1,0:T(8,128)(2,1)S(1)}, bf16[64,2048]{1,0:T(8,128)(2,1)S(1)}, u32[]{:S(2)}, u32[]{:S(2)}) collective-permute-start(bf16[64,2048]{1,0:T(8,128)(2,1)S(1)} %constant_dynamic-slice_fusion), channel_id=1, source_target_pairs={{0,2},{1,3},{2,0},{3,1},{4,6},{5,7},{6,4},{7,5},{8,10},{9,11},{10,... | collective-permute-start | bytes 786440 | tf_op jit(solution)/shard_map/ppermute | solution.py:330
  13.0 70.9 %copy-start.4 = (s32[512]{0:T(512)S(1)}, s32[512]{0:T(512)}, u32[]{:S(2)}) copy-start(s32[512]{0:T(512)} %param.10) | copy-start | bytes 6148
  13.0 70.9 %copy-start.3 = (f32[3,512]{1,0:T(4,128)S(1)}, f32[3,512]{1,0:T(4,128)}, u32[]{:S(2)}) copy-start(f32[3,512]{1,0:T(4,128)} %param.9) | copy-start | bytes 18436
  14.7 89.9 %copy-start = (bf16[512,2048]{1,0:T(8,128)(2,1)S(1)}, bf16[512,2048]{1,0:T(8,128)(2,1)}, u32[]{:S(2)}) copy-start(bf16[512,2048]{1,0:T(8,128)(2,1)} %refs_9_.1) | copy-start | bytes 6291460
  14.7 89.9 %copy-start.1 = (f32[2048]{0:T(1024)S(1)}, f32[2048]{0:T(1024)}, u32[]{:S(2)}) copy-start(f32[2048]{0:T(1024)} %param.8) | copy-start | bytes 24580
  14.7 89.9 %copy-start.2 = (s32[2]{0:T(128)S(1)}, s32[2]{0:T(128)}, u32[]{:S(2)}) copy-start(s32[2]{0:T(128)} %pad_add_fusion.place.refs_0_) | copy-start | bytes 28
  31.3 63.5 %all-to-all-start = ((s16[32,128,128]{2,1,0:T(8,128)(2,1)}), s16[32,128,128]{2,1,0:T(8,128)(2,1)S(1)}, u32[]{:S(2)}, u32[]{:S(2)}) async-start(s16[32,128,128]{2,1,0:T(8,128)(2,1)} %enter.1), calls=%async_computation | async-start | bytes 2097152 | tf_op jit(solution)/shard_map/all_to_all | solution.py:377
  35.2 33.3 %collective-permute-start.13 = (bf16[192,2048]{1,0:T(8,128)(2,1)}, bf16[192,2048]{1,0:T(8,128)(2,1)}, u32[]{:S(2)}, u32[]{:S(2)}) collective-permute-start(bf16[192,2048]{1,0:T(8,128)(2,1)} %constant_dynamic-update-slice_fusion.refs_10_), channel_id=1, source_target_pairs={{0,24},{4,28},{8,16},{12,20},{16,8},{20,12},{24,0},{28,4},{1,25},{... | collective-permute-start | bytes 2359304 | tf_op jit(solution)/shard_map/ppermute | solution.py:333
  38.0 45.5 %collective-permute-start.11 = (bf16[192,2048]{1,0:T(8,128)(2,1)}, bf16[192,2048]{1,0:T(8,128)(2,1)}, u32[]{:S(2)}, u32[]{:S(2)}) collective-permute-start(bf16[192,2048]{1,0:T(8,128)(2,1)} %constant_dynamic-update-slice_fusion.refs_10_), channel_id=1, source_target_pairs={{0,16},{4,20},{8,24},{12,28},{16,0},{20,4},{24,8},{28,12},{1,17},{... | collective-permute-start | bytes 2359304 | tf_op jit(solution)/shard_map/ppermute | solution.py:333
  38.5 45.4 %collective-permute-start.9 = (bf16[192,2048]{1,0:T(8,128)(2,1)}, bf16[192,2048]{1,0:T(8,128)(2,1)}, u32[]{:S(2)}, u32[]{:S(2)}) collective-permute-start(bf16[192,2048]{1,0:T(8,128)(2,1)} %constant_dynamic-update-slice_fusion.refs_10_), channel_id=1, source_target_pairs={{0,8},{4,12},{8,0},{12,4},{16,24},{20,28},{24,16},{28,20},{1,9},{5... | collective-permute-start | bytes 2359304 | tf_op jit(solution)/shard_map/ppermute | solution.py:333
  38.8 60.0 %collective-permute-start.8 = (bf16[192,2048]{1,0:T(8,128)(2,1)}, bf16[192,2048]{1,0:T(8,128)(2,1)}, u32[]{:S(2)}, u32[]{:S(2)}) collective-permute-start(bf16[192,2048]{1,0:T(8,128)(2,1)} %constant_dynamic-update-slice_fusion.refs_10_), channel_id=1, source_target_pairs={{0,4},{4,0},{8,12},{12,8},{16,20},{20,16},{24,28},{28,24},{1,5},{5... | collective-permute-start | bytes 2359304 | tf_op jit(solution)/shard_map/ppermute | solution.py:333
  68.5 30.8 %collective-permute-start.14 = (bf16[192,2048]{1,0:T(8,128)(2,1)}, bf16[192,2048]{1,0:T(8,128)(2,1)}, u32[]{:S(2)}, u32[]{:S(2)}) collective-permute-start(bf16[192,2048]{1,0:T(8,128)(2,1)} %collective-permute-done.13.refs_16_), channel_id=1, source_target_pairs={{0,4},{4,0},{8,12},{12,8},{16,20},{20,16},{24,28},{28,24},{1,5},{5... | collective-permute-start | bytes 2359304 | tf_op jit(solution)/shard_map/ppermute | solution.py:333
  83.4 15.9 %collective-permute-start.12 = (bf16[192,2048]{1,0:T(8,128)(2,1)}, bf16[192,2048]{1,0:T(8,128)(2,1)}, u32[]{:S(2)}, u32[]{:S(2)}) collective-permute-start(bf16[192,2048]{1,0:T(8,128)(2,1)} %collective-permute-done.11.refs_14_), channel_id=1, source_target_pairs={{0,4},{4,0},{8,12},{12,8},{16,20},{20,16},{24,28},{28,24},{1,5},{5... | collective-permute-start | bytes 2359304 | tf_op jit(solution)/shard_map/ppermute | solution.py:333
  83.9 15.4 %collective-permute-start.10 = (bf16[192,2048]{1,0:T(8,128)(2,1)}, bf16[192,2048]{1,0:T(8,128)(2,1)}, u32[]{:S(2)}, u32[]{:S(2)}) collective-permute-start(bf16[192,2048]{1,0:T(8,128)(2,1)} %collective-permute-done.9.refs_12_), channel_id=1, source_target_pairs={{0,4},{4,0},{8,12},{12,8},{16,20},{20,16},{24,28},{28,24},{1,5},{5... | collective-permute-start | bytes 2359304 | tf_op jit(solution)/shard_map/ppermute | solution.py:333
  83.9 4.6 %collective-permute-start.7 = (f32[4,512]{1,0:T(4,128)S(1)}, f32[4,512]{1,0:T(4,128)S(1)}, u32[]{:S(2)}, u32[]{:S(2)}) collective-permute-start(f32[4,512]{1,0:T(4,128)S(1)} %pad_maximum_fusion.refs_5_), channel_id=1, source_target_pairs={{0,3},{1,0},{2,1},{3,2},{4,7},{5,4},{6,5},{7,6},{8,11},{9,8},{10,9... | collective-permute-start | bytes 24584 | tf_op jit(solution)/shard_map/ppermute | solution.py:362
  88.5 4.5 %collective-permute-start.6 = (f32[4,512]{1,0:T(4,128)S(1)}, f32[4,512]{1,0:T(4,128)S(1)}, u32[]{:S(2)}, u32[]{:S(2)}) collective-permute-start(f32[4,512]{1,0:T(4,128)S(1)} %pad_maximum_fusion.refs_5_), channel_id=1, source_target_pairs={{0,2},{1,3},{2,0},{3,1},{4,6},{5,7},{6,4},{7,5},{8,10},{9,11},{10,... | collective-permute-start | bytes 24584 | tf_op jit(solution)/shard_map/ppermute | solution.py:362
  93.1 5.7 %collective-permute-start.5 = (f32[4,512]{1,0:T(4,128)S(1)}, f32[4,512]{1,0:T(4,128)S(1)}, u32[]{:S(2)}, u32[]{:S(2)}) collective-permute-start(f32[4,512]{1,0:T(4,128)S(1)} %pad_maximum_fusion.refs_5_), channel_id=1, source_target_pairs={{0,1},{1,2},{2,3},{3,0},{4,5},{5,6},{6,7},{7,4},{8,9},{9,10},{10,1... | collective-permute-start | bytes 24584 | tf_op jit(solution)/shard_map/ppermute | solution.py:362
  98.8 3.9 %collective-permute-start.4 = (s16[32,4,8,128]{3,2,1,0:T(8,128)(2,1)S(1)}, s16[32,4,8,128]{3,2,1,0:T(8,128)(2,1)S(1)}, u32[]{:S(2)}, u32[]{:S(2)}) collective-permute-start(s16[32,4,8,128]{3,2,1,0:T(8,128)(2,1)S(1)} %get-tuple-element.28), channel_id=1, source_target_pairs={{4,0},{1,4},{5,1},{2,5},{6,2},{3,6},{7,3},{11,7},{15,11},{10,15},{... | collective-permute-start | bytes 786440 | tf_op jit(solution)/shard_map/ppermute | solution.py:393
  98.8 5.8 %collective-permute-start.3 = (s16[32,4,8,128]{3,2,1,0:T(8,128)(2,1)S(1)}, s16[32,4,8,128]{3,2,1,0:T(8,128)(2,1)S(1)}, u32[]{:S(2)}, u32[]{:S(2)}) collective-permute-start(s16[32,4,8,128]{3,2,1,0:T(8,128)(2,1)S(1)} %get-tuple-element.29), channel_id=1, source_target_pairs={{0,4},{4,1},{1,5},{5,2},{2,6},{6,3},{3,7},{7,11},{11,15},{15,10},{... | collective-permute-start | bytes 786440 | tf_op jit(solution)/shard_map/ppermute | solution.py:392
  114.3 5.8 %collective-permute-start.15 = (bf16[64,2048]{1,0:T(8,128)(2,1)S(1)}, bf16[64,2048]{1,0:T(8,128)(2,1)S(1)}, u32[]{:S(2)}, u32[]{:S(2)}) collective-permute-start(bf16[64,2048]{1,0:T(8,128)(2,1)S(1)} %get-tuple-element.18), channel_id=1, source_target_pairs={{0,4},{4,1},{1,5},{5,2},{2,6},{6,3},{3,7},{7,11},{11,15},{15,10},{... | collective-permute-start | bytes 786440 | tf_op jit(solution)/shard_map/ppermute | solution.py:392
  114.4 5.8 %collective-permute-start.16 = (bf16[64,2048]{1,0:T(8,128)(2,1)S(1)}, bf16[64,2048]{1,0:T(8,128)(2,1)S(1)}, u32[]{:S(2)}, u32[]{:S(2)}) collective-permute-start(bf16[64,2048]{1,0:T(8,128)(2,1)S(1)} %get-tuple-element.19), channel_id=1, source_target_pairs={{4,0},{1,4},{5,1},{2,5},{6,2},{3,6},{7,3},{11,7},{15,11},{10,15},{... | collective-permute-start | bytes 786440 | tf_op jit(solution)/shard_map/ppermute | solution.py:393
  125.4 5.9 %collective-permute-start.17 = (bf16[64,2048]{1,0:T(8,128)(2,1)S(1)}, bf16[64,2048]{1,0:T(8,128)(2,1)S(1)}, u32[]{:S(2)}, u32[]{:S(2)}) collective-permute-start(bf16[64,2048]{1,0:T(8,128)(2,1)S(1)} %get-tuple-element.24), channel_id=1, source_target_pairs={{0,4},{4,1},{1,5},{5,2},{2,6},{6,3},{3,7},{7,11},{11,15},{15,10},{... | collective-permute-start | bytes 786440 | tf_op jit(solution)/shard_map/ppermute | solution.py:392
  126.7 4.5 %collective-permute-start.18 = (bf16[64,2048]{1,0:T(8,128)(2,1)S(1)}, bf16[64,2048]{1,0:T(8,128)(2,1)S(1)}, u32[]{:S(2)}, u32[]{:S(2)}) collective-permute-start(bf16[64,2048]{1,0:T(8,128)(2,1)S(1)} %get-tuple-element.25), channel_id=1, source_target_pairs={{4,0},{1,4},{5,1},{2,5},{6,2},{3,6},{7,3},{11,7},{15,11},{10,15},{... | collective-permute-start | bytes 786440 | tf_op jit(solution)/shard_map/ppermute | solution.py:393
